TPU v7x, 512 devices: a whole 4x8x8 slice. The times are simulated.
512 devices in a mesh: proj: 16 (over z_hi, x, core), scen: 32 (over y, z_lo).
Axes of the slice: x: 4, y: 8, z: 8 (z_hi: 2, z_lo: 4; z = z_hi * 4 + z_lo), core: 2. Of those that a mesh axis runs over, the one named last changes fastest.
Arguments:
- fund_value: float32 [16384, 4096], P('proj', 'scen'), may hold values from 0.5 to 2
- in_force: float32 [16384, 4096], P('proj', 'scen'), may hold values from 0.5 to 1.5
- guarantee_base: float32 [16384, 4096], P('proj', 'scen'), may hold values from 0.5 to 2
- lapse_rate: float32 [16384, 4096], P('proj', 'scen'), may hold values from 0.02 to 0.4
- cohort: int32 [16384], P('proj'), may hold values from 0 to 511, as said below
- product: int32 [16384], P('proj'), may hold values from 0 to 15
- guarantee_type: int32 [16384], P('proj'), may hold values from 0 to 3
- returns: float32 [8, 12, 4096], P(None, None, 'scen'), may hold values from -0.625 to 0.625
- mix_table: float32 [16, 8], replicated, may hold values from 0.05 to 1
- fee_table: float32 [4], replicated, may hold values from 0.001 to 0.01
- rollup_table: float32 [4], replicated, may hold values from 0.01 to 0.08
- fund_vol: float32 [8], replicated, may hold values from 0.15 to 0.6
- closing_sigma_figure: float32 [4096], P('scen'), may hold values from 0.5 to 2
- shocks: float32 [8, 2, 1024], P(None, None, 'scen'), may hold values from -6 to 6
- base_table: float32 [10, 16], replicated, may hold values from 0.03 to 0.2
- year_index: int32 [1], replicated, may hold values from 0 to 9
Outputs:
- fund_next: float32 [16384, 4096], P('proj', 'scen')
- force_next: float32 [16384, 4096], P('proj', 'scen')
- base_next: float32 [16384, 4096], P('proj', 'scen')
- lapse_next: float32 [16384, 4096], P('proj', 'scen')
- benefit_cost_per_account: float32 [512, 4096], P('proj', 'scen')
Inputs may be any that keep to these rules, and one draw needn't show every extreme that they name: Each cohort holds exactly 32 model points; the model points of each index of proj include exactly 64 whose cohorts lie in the block of 32 cohorts that any one index of proj owns (cohorts q * 32 onward for index q).
All inputs are finite; a program needn't handle non-finite values.
Results may differ from a plain program's by a relative error of at most 0.00026.
Values sent between devices are 32-bit elements; how exact they have to be, the bound alone decides.
A program may use at most 64 MiB of HBM per device.

v0:
```python
import math

import jax
import jax.numpy as jnp
from jax import lax
from jax.sharding import PartitionSpec as P

COHORTS = 512


HIGHEST = lax.Precision.HIGHEST
discount_rate = 0.96
lapse_floor = 0.3
lapse_span = 2.0
lapse_slope = 5.0
lapse_pivot = 0.4


def sent_to_all(value, axis):
    copies = jnp.broadcast_to(value, (lax.axis_size(axis), *value.shape))
    return lax.all_to_all(copies, axis, split_axis=0, concat_axis=0, tiled=True)


def in_order(tiles, dim):
    shape = list(tiles.shape[1:])
    shape[dim] *= tiles.shape[0]
    return jnp.moveaxis(tiles, 0, dim).reshape(shape)


def gathered_copies(value, axis, dim):
    tiles = sent_to_all(value, axis)
    return in_order(tiles, dim)


def project(
    fund_value, in_force, guarantee_base, lapse_rate, mix_rows, fee_rows, rollup_rows, returns
):
    keep_fee = (1.0 - fee_rows)[:, None]
    rollup_month = (1.0 + rollup_rows / 12.0)[:, None]
    survive = 1.0 - lapse_rate / 12.0
    for month_step in range(returns.shape[1]):
        growth = 1.0 + jnp.dot(
            mix_rows,
            returns[:, month_step, :],
            precision=HIGHEST,
            preferred_element_type=jnp.float32,
        )
        fund_value = fund_value * growth * keep_fee
        guarantee_base = jnp.maximum(guarantee_base * rollup_month, fund_value)
        in_force = in_force * survive
    return (fund_value, in_force, guarantee_base)


def price_rows(scenario_conditions, sigma_figures, embedded_trials):
    factor_count, horizon_count, path_count = embedded_trials.shape
    span_cols = horizon_count * path_count
    flat_paths = embedded_trials.reshape(factor_count, span_cols)
    horizon = jnp.repeat(jnp.arange(1, horizon_count + 1, dtype=jnp.float32), path_count)
    weights = discount_rate**horizon
    entry_number_overall = scenario_conditions.shape[1]
    target = max(1, (1 << 20) // span_cols)
    block_rows = math.gcd(entry_number_overall, 1 << target.bit_length() - 1)
    block_count = entry_number_overall // block_rows
    benefit_strike_share = scenario_conditions[0].reshape(block_count, block_rows)
    fund_loads = scenario_conditions[1:]
    distributed_amounts = jnp.sum(fund_loads * fund_loads, axis=0).reshape(block_count, block_rows)
    cohort_sorted_entries = fund_loads.reshape(factor_count, block_count, block_rows).transpose(
        1, 0, 2
    )
    sigma_entries = sigma_figures.reshape(block_count, block_rows)

    def valuation_batch(fragment_list):
        money_rows, load_rows, level_part, spread_rows = fragment_list
        shifted = lax.dot_general(
            flat_paths,
            load_rows,
            (((0,), (0,)), ((), ())),
            precision=HIGHEST,
            preferred_element_type=jnp.float32,
        )
        exponent = (
            level_part[None, :] * shifted
            - 0.5 * (level_part * level_part)[None, :] * horizon[:, None] * spread_rows[None, :]
        )
        payoff = jnp.maximum(money_rows[None, :] - jnp.exp(exponent), 0.0)
        return jnp.dot(weights, payoff, precision=HIGHEST)

    valued_amounts = lax.map(
        valuation_batch,
        (benefit_strike_share, cohort_sorted_entries, sigma_entries, distributed_amounts),
    )
    return valued_amounts.reshape(entry_number_overall)


def valuation_conditions(scenario_conditions, sigma_figures, embedded_trials):
    cohort_count, columns, scen_count = scenario_conditions.shape
    flat_states = scenario_conditions.transpose(1, 2, 0).reshape(columns, scen_count * cohort_count)
    sigma_entries = jnp.repeat(sigma_figures, cohort_count)
    return price_rows(flat_states, sigma_entries, embedded_trials).reshape(scen_count, cohort_count)


def build_features(weighted, secured, mix_rows):
    features = jnp.concatenate(
        [weighted[:, None, :], secured[:, None, :], weighted[:, None, :] * mix_rows[:, :, None]],
        axis=1,
    )
    return (features, features.reshape(features.shape[0], features.shape[1] * features.shape[2]))


def body(
    fund_value,
    in_force,
    guarantee_base,
    lapse_rate,
    cohort,
    product,
    guarantee_type,
    returns,
    mix_table,
    fee_table,
    rollup_table,
    fund_vol,
    closing_sigma_figure,
    shocks,
    base_table,
    year_index,
):
    product_count = mix_table.shape[0]
    mix_norm = mix_table / jnp.sum(mix_table, axis=1, keepdims=True)
    product_hot = (product[:, None] == jnp.arange(product_count, dtype=jnp.int32)[None, :]).astype(
        jnp.float32
    )
    type_hot = (
        guarantee_type[:, None] == jnp.arange(fee_table.shape[0], dtype=jnp.int32)[None, :]
    ).astype(jnp.float32)
    mix_rows = jnp.dot(product_hot, mix_norm, precision=HIGHEST, preferred_element_type=jnp.float32)
    fee_rows = jnp.dot(type_hot, fee_table, precision=HIGHEST, preferred_element_type=jnp.float32)
    rollup_rows = jnp.dot(
        type_hot, rollup_table, precision=HIGHEST, preferred_element_type=jnp.float32
    )
    fund_next, force_next, base_next = project(
        fund_value, in_force, guarantee_base, lapse_rate, mix_rows, fee_rows, rollup_rows, returns
    )
    weighted = force_next * fund_next
    secured = force_next * base_next
    owned = COHORTS // lax.axis_size("proj")
    scen_cols = weighted.shape[1]
    owner = cohort // owned
    order = jnp.argsort(owner, stable=True)
    payload = jnp.concatenate([weighted, secured], axis=1)[order]
    labels = (cohort % owned * product_count + product)[order].astype(jnp.float32)
    arrived, arrived_labels = (
        lax.all_to_all(payload, "proj", split_axis=0, concat_axis=0, tiled=True),
        lax.all_to_all(labels, "proj", split_axis=0, concat_axis=0, tiled=True),
    )
    label_ints = arrived_labels.astype(jnp.int32)
    local_cohort = label_ints // product_count
    local_product = label_ints % product_count
    arrived_hot = (
        local_product[:, None] == jnp.arange(product_count, dtype=jnp.int32)[None, :]
    ).astype(jnp.float32)
    arrived_mix = jnp.dot(
        arrived_hot, mix_norm, precision=HIGHEST, preferred_element_type=jnp.float32
    )
    features, flat_features = build_features(
        arrived[:, :scen_cols], arrived[:, scen_cols:], arrived_mix
    )
    member = (jnp.arange(owned, dtype=jnp.int32)[:, None] == local_cohort[None, :]).astype(
        jnp.float32
    )
    totals = jnp.dot(
        member, flat_features, precision=HIGHEST, preferred_element_type=jnp.float32
    ).reshape(owned, features.shape[1], scen_cols)
    value_sum = totals[:, 0]
    guarantee_sum = totals[:, 1]
    scenario_conditions = jnp.concatenate(
        [
            (guarantee_sum / value_sum)[:, None, :],
            totals[:, 2:] / value_sum[:, None, :] * fund_vol[None, :, None],
        ],
        axis=1,
    )
    embedded_trials = jnp.cumsum(shocks, axis=1)
    every_valuation_trial = gathered_copies(embedded_trials, "scen", 2)
    valued_amounts = valuation_conditions(
        scenario_conditions, closing_sigma_figure, every_valuation_trial
    )
    benefit_cost_per_account = valued_amounts.T / every_valuation_trial.shape[2]
    every_cost = gathered_copies(benefit_cost_per_account, "proj", 0)
    cost_rows = every_cost[cohort]
    year_row = lax.dynamic_slice_in_dim(base_table, year_index[0], 1, 0)[0]
    base_lapse = jnp.dot(
        product_hot, year_row, precision=HIGHEST, preferred_element_type=jnp.float32
    )
    lapse_next = base_lapse[:, None] * (
        lapse_floor + lapse_span * jax.nn.sigmoid(lapse_slope * (lapse_pivot - cost_rows))
    )
    return (fund_next, force_next, base_next, lapse_next, benefit_cost_per_account)


def solution(mesh):
    placed = (
        P("proj", "scen"),
        P("proj", "scen"),
        P("proj", "scen"),
        P("proj", "scen"),
        P("proj"),
        P("proj"),
        P("proj"),
        P(None, None, "scen"),
        P(),
        P(),
        P(),
        P(),
        P("scen"),
        P(None, None, "scen"),
        P(),
        P(),
    )
    return jax.shard_map(
        body,
        mesh=mesh,
        in_specs=placed,
        out_specs=(
            P("proj", "scen"),
            P("proj", "scen"),
            P("proj", "scen"),
            P("proj", "scen"),
            P("proj", "scen"),
        ),
        check_vma=False,
    )
```

profile of v0, /device:TPU:1, one launch (start us, length us, event | category | flops | bytes accessed | tf_op | source)
XLA Modules:
  0.0 201.9 jit_solution(2341737875824705488)
XLA Ops:
  1.5 4.4 %sort.17 = (s32[1024]{0:T(1024)}, s32[1024]{0:T(1024)S(1)}) sort(s32[1024]{0:T(1024)S(1)} %get-tuple-element.158, s32[1024]{0:T(1024)S(1)} %iota.22), dimensions={0}, to_apply=%region_1.2 | sort | flops 10240 | bytes 16384 | tf_op jit(solution)/shard_map/jit(argsort)/sort | solution.py:149
  5.9 4.5 %gather_fusion = s32[1024]{0:T(1024)S(1)} fusion(s32[1024]{0:T(1024)S(1)} %get-tuple-element.157, s32[1024]{0:T(1024)S(1)} %fusion.66), kind=kCustom, calls=%fused_computation | custom fusion | bytes 12288 | tf_op jit(solution)/shard_map/gather | solution.py:151
  11.1 14.2 %all-to-all-start = ((f32[16,64,1]{1,2,0:T(1,128)}), f32[16,64,1]{1,2,0:T(1,128)S(1)}, u32[]{:S(2)}, u32[]{:S(2)}) async-start(f32[16,64,1]{1,2,0:T(1,128)} %bitcast.20), calls=%async_computation | async-start | bytes 16384 | tf_op jit(solution)/shard_map/all_to_all | solution.py:154
  51.4 9.9 %all-to-all-start.2 = ((f32[32,1,512]{2,1,0:T(1,128)}), f32[32,1,512]{2,1,0:T(1,128)S(1)}, u32[]{:S(2)}, u32[]{:S(2)}) async-start(f32[32,1,512]{2,1,0:T(1,128)} %reshape.149), calls=%async_computation.2 | async-start | bytes 131072 | tf_op jit(solution)/shard_map/all_to_all | solution.py:21
  63.0 4.7 %gather_fusion.1 = f32[1024,256]{1,0:T(8,128)} fusion(f32[1024,256]{1,0:T(8,128)S(1)} %copy.74, s32[1024]{0:T(1024)S(1)} %fusion.66), kind=kCustom, calls=%fused_computation.1 | custom fusion | bytes 2101248 | tf_op jit(solution)/shard_map/gather | solution.py:150
  70.7 11.1 %all-to-all-start.1 = ((f32[16,64,256]{2,1,0:T(8,128)}), f32[16,64,256]{2,1,0:T(8,128)S(1)}, u32[]{:S(2)}, u32[]{:S(2)}) async-start(f32[16,64,256]{2,1,0:T(8,128)} %bitcast.22), calls=%async_computation.1 | async-start | bytes 2097152 | tf_op jit(solution)/shard_map/all_to_all | solution.py:153
  84.5 23.8 %all-to-all-done.1 = f32[16,64,256]{2,1,0:T(8,128)S(1)} async-done(((f32[16,64,256]{2,1,0:T(8,128)}), f32[16,64,256]{2,1,0:T(8,128)S(1)}, u32[]{:S(2)}, u32[]{:S(2)}) %all-to-all-start.1) | async-done | bytes 1048608 | tf_op jit(solution)/shard_map/all_to_all | solution.py:153
  113.0 68.1 %while.11 = (s32[]{:T(128)}, f32[8,512]{1,0:T(8,128)S(1)}, f32[8,512]{1,0:T(8,128)S(1)}, f32[8,512]{1,0:T(8,128)S(1)}, f32[8,8,512]{2,0,1:T(8,128)S(1)}, /*index...) while((s32[]{:T(128)}, f32[8,512]{1,0:T(8,128)S(1)}, ...), condition=%wide.region_5.6_spmd.clone, body=%wide.region_4.5_spmd.clone.sunk | while | flops 119538688 | bytes 8597645 | solution.py:88
  113.1 3.5 %fusion.126 = f32[512,2048]{1,0:T(8,128)S(1)} fusion(f32[8,2048]{1,0:T(8,128)S(1)} %get-tuple-element.252, f32[1,8,512]{2,0,1:T(1,128)S(1)} %constant_dynamic-slice_fusion.7), kind=kOutput, calls=%fused_computation.20.clone.1 | convolution fusion | flops 100663296 | bytes 4276224 | tf_op jit(solution)/shard_map/while/body/eval_jaxpr/dot_general | solution.py:74
  116.8 4.7 %fusion.127 = f32[1,512]{1,0:T(1,128)S(1)} fusion(f32[2048,1]{0,1:T(1,128)S(1)} %bitcast.152, f32[512,2048]{1,0:T(8,128)S(1)} %fusion.126, f32[512]{0:T(512)S(1)} %bitcast.157, f32[2048]{0:T(1024)S(1)} %bitcast.153, f32[512]{0:T(512)S(1)} %bitcast.155, f32[512]{0:T(512)S(1)} %bitcast.156, f32[512]{0:T(512)S(1)} %bitcast.154), kind=kOutput, calls=%fused_computation.9.clone.1 | convolution fusion | flops 18874368 | bytes 4220928 | tf_op jit(solution)/shard_map/while/body/eval_jaxpr/dot_general | solution.py:86
  121.6 3.5 %fusion.126 = f32[512,2048]{1,0:T(8,128)S(1)} fusion(f32[8,2048]{1,0:T(8,128)S(1)} %get-tuple-element.252, f32[1,8,512]{2,0,1:T(1,128)S(1)} %constant_dynamic-slice_fusion.7), kind=kOutput, calls=%fused_computation.20.clone.1 | convolution fusion | flops 100663296 | bytes 4276224 | tf_op jit(solution)/shard_map/while/body/eval_jaxpr/dot_general | solution.py:74
  125.3 4.7 %fusion.127 = f32[1,512]{1,0:T(1,128)S(1)} fusion(f32[2048,1]{0,1:T(1,128)S(1)} %bitcast.152, f32[512,2048]{1,0:T(8,128)S(1)} %fusion.126, f32[512]{0:T(512)S(1)} %bitcast.157, f32[2048]{0:T(1024)S(1)} %bitcast.153, f32[512]{0:T(512)S(1)} %bitcast.155, f32[512]{0:T(512)S(1)} %bitcast.156, f32[512]{0:T(512)S(1)} %bitcast.154), kind=kOutput, calls=%fused_computation.9.clone.1 | convolution fusion | flops 18874368 | bytes 4220928 | tf_op jit(solution)/shard_map/while/body/eval_jaxpr/dot_general | solution.py:86
  133.8 4.7 %fusion.127 = f32[1,512]{1,0:T(1,128)S(1)} fusion(f32[2048,1]{0,1:T(1,128)S(1)} %bitcast.152, f32[512,2048]{1,0:T(8,128)S(1)} %fusion.126, f32[512]{0:T(512)S(1)} %bitcast.157, f32[2048]{0:T(1024)S(1)} %bitcast.153, f32[512]{0:T(512)S(1)} %bitcast.155, f32[512]{0:T(512)S(1)} %bitcast.156, f32[512]{0:T(512)S(1)} %bitcast.154), kind=kOutput, calls=%fused_computation.9.clone.1 | convolution fusion | flops 18874368 | bytes 4220928 | tf_op jit(solution)/shard_map/while/body/eval_jaxpr/dot_general | solution.py:86
  138.6 3.5 %fusion.126 = f32[512,2048]{1,0:T(8,128)S(1)} fusion(f32[8,2048]{1,0:T(8,128)S(1)} %get-tuple-element.252, f32[1,8,512]{2,0,1:T(1,128)S(1)} %constant_dynamic-slice_fusion.7), kind=kOutput, calls=%fused_computation.20.clone.1 | convolution fusion | flops 100663296 | bytes 4276224 | tf_op jit(solution)/shard_map/while/body/eval_jaxpr/dot_general | solution.py:74
  142.3 4.7 %fusion.127 = f32[1,512]{1,0:T(1,128)S(1)} fusion(f32[2048,1]{0,1:T(1,128)S(1)} %bitcast.152, f32[512,2048]{1,0:T(8,128)S(1)} %fusion.126, f32[512]{0:T(512)S(1)} %bitcast.157, f32[2048]{0:T(1024)S(1)} %bitcast.153, f32[512]{0:T(512)S(1)} %bitcast.155, f32[512]{0:T(512)S(1)} %bitcast.156, f32[512]{0:T(512)S(1)} %bitcast.154), kind=kOutput, calls=%fused_computation.9.clone.1 | convolution fusion | flops 18874368 | bytes 4220928 | tf_op jit(solution)/shard_map/while/body/eval_jaxpr/dot_general | solution.py:86
  147.1 3.5 %fusion.126 = f32[512,2048]{1,0:T(8,128)S(1)} fusion(f32[8,2048]{1,0:T(8,128)S(1)} %get-tuple-element.252, f32[1,8,512]{2,0,1:T(1,128)S(1)} %constant_dynamic-slice_fusion.7), kind=kOutput, calls=%fused_computation.20.clone.1 | convolution fusion | flops 100663296 | bytes 4276224 | tf_op jit(solution)/shard_map/while/body/eval_jaxpr/dot_general | solution.py:74
  150.8 4.7 %fusion.127 = f32[1,512]{1,0:T(1,128)S(1)} fusion(f32[2048,1]{0,1:T(1,128)S(1)} %bitcast.152, f32[512,2048]{1,0:T(8,128)S(1)} %fusion.126, f32[512]{0:T(512)S(1)} %bitcast.157, f32[2048]{0:T(1024)S(1)} %bitcast.153, f32[512]{0:T(512)S(1)} %bitcast.155, f32[512]{0:T(512)S(1)} %bitcast.156, f32[512]{0:T(512)S(1)} %bitcast.154), kind=kOutput, calls=%fused_computation.9.clone.1 | convolution fusion | flops 18874368 | bytes 4220928 | tf_op jit(solution)/shard_map/while/body/eval_jaxpr/dot_general | solution.py:86
  155.6 3.5 %fusion.126 = f32[512,2048]{1,0:T(8,128)S(1)} fusion(f32[8,2048]{1,0:T(8,128)S(1)} %get-tuple-element.252, f32[1,8,512]{2,0,1:T(1,128)S(1)} %constant_dynamic-slice_fusion.7), kind=kOutput, calls=%fused_computation.20.clone.1 | convolution fusion | flops 100663296 | bytes 4276224 | tf_op jit(solution)/shard_map/while/body/eval_jaxpr/dot_general | solution.py:74
  159.3 4.7 %fusion.127 = f32[1,512]{1,0:T(1,128)S(1)} fusion(f32[2048,1]{0,1:T(1,128)S(1)} %bitcast.152, f32[512,2048]{1,0:T(8,128)S(1)} %fusion.126, f32[512]{0:T(512)S(1)} %bitcast.157, f32[2048]{0:T(1024)S(1)} %bitcast.153, f32[512]{0:T(512)S(1)} %bitcast.155, f32[512]{0:T(512)S(1)} %bitcast.156, f32[512]{0:T(512)S(1)} %bitcast.154), kind=kOutput, calls=%fused_computation.9.clone.1 | convolution fusion | flops 18874368 | bytes 4220928 | tf_op jit(solution)/shard_map/while/body/eval_jaxpr/dot_general | solution.py:86
  167.8 4.7 %fusion.127 = f32[1,512]{1,0:T(1,128)S(1)} fusion(f32[2048,1]{0,1:T(1,128)S(1)} %bitcast.152, f32[512,2048]{1,0:T(8,128)S(1)} %fusion.126, f32[512]{0:T(512)S(1)} %bitcast.157, f32[2048]{0:T(1024)S(1)} %bitcast.153, f32[512]{0:T(512)S(1)} %bitcast.155, f32[512]{0:T(512)S(1)} %bitcast.156, f32[512]{0:T(512)S(1)} %bitcast.154), kind=kOutput, calls=%fused_computation.9.clone.1 | convolution fusion | flops 18874368 | bytes 4220928 | tf_op jit(solution)/shard_map/while/body/eval_jaxpr/dot_general | solution.py:86
  172.6 3.5 %fusion.126 = f32[512,2048]{1,0:T(8,128)S(1)} fusion(f32[8,2048]{1,0:T(8,128)S(1)} %get-tuple-element.252, f32[1,8,512]{2,0,1:T(1,128)S(1)} %constant_dynamic-slice_fusion.7), kind=kOutput, calls=%fused_computation.20.clone.1 | convolution fusion | flops 100663296 | bytes 4276224 | tf_op jit(solution)/shard_map/while/body/eval_jaxpr/dot_general | solution.py:74
  176.3 4.7 %fusion.127 = f32[1,512]{1,0:T(1,128)S(1)} fusion(f32[2048,1]{0,1:T(1,128)S(1)} %bitcast.152, f32[512,2048]{1,0:T(8,128)S(1)} %fusion.126, f32[512]{0:T(512)S(1)} %bitcast.157, f32[2048]{0:T(1024)S(1)} %bitcast.153, f32[512]{0:T(512)S(1)} %bitcast.155, f32[512]{0:T(512)S(1)} %bitcast.156, f32[512]{0:T(512)S(1)} %bitcast.154), kind=kOutput, calls=%fused_computation.9.clone.1 | convolution fusion | flops 18874368 | bytes 4220928 | tf_op jit(solution)/shard_map/while/body/eval_jaxpr/dot_general | solution.py:86
  182.0 4.4 %all-to-all-start.3 = ((f32[16,32,128]{2,1,0:T(8,128)}), f32[16,32,128]{2,1,0:T(8,128)S(1)}, u32[]{:S(2)}, u32[]{:S(2)}) async-start(f32[16,32,128]{2,1,0:T(8,128)} %broadcast_in_dim.68), calls=%async_computation.3 | async-start | bytes 524288 | tf_op jit(solution)/shard_map/all_to_all | solution.py:21
  190.5 7.2 %all-to-all-done.3 = f32[16,32,128]{2,1,0:T(8,128)S(1)} async-done(((f32[16,32,128]{2,1,0:T(8,128)}), f32[16,32,128]{2,1,0:T(8,128)S(1)}, u32[]{:S(2)}, u32[]{:S(2)}) %all-to-all-start.3) | async-done | bytes 262176 | tf_op jit(solution)/shard_map/all_to_all | solution.py:21
  (197 shorter events, 56.7 us)
Async XLA Ops:
  0.6 189.4 %copy-start = (f32[10,16]{1,0:T(8,128)S(1)}, f32[10,16]{1,0:T(8,128)}, u32[]{:S(2)}) copy-start(f32[10,16]{1,0:T(8,128)} %param.32) | copy-start | bytes 1924
  0.6 24.7 %copy-start.20 = (s32[1024]{0:T(1024)S(1)}, s32[1024]{0:T(1024)}, u32[]{:S(2)}) copy-start(s32[1024]{0:T(1024)} %param.23) | copy-start | bytes 12292
  0.7 24.7 %copy-start.21 = (f32[16,8]{0,1:T(8,128)S(1)}, f32[16,8]{0,1:T(8,128)}, u32[]{:S(2)}) copy-start(f32[16,8]{0,1:T(8,128)} %param.26) | copy-start | bytes 1540
  0.7 25.1 %copy-start.24 = (s32[1024]{0:T(1024)S(1)}, s32[1024]{0:T(1024)}, u32[]{:S(2)}) copy-start(s32[1024]{0:T(1024)} %param.24) | copy-start | bytes 12292
  0.7 25.1 %copy-start.25 = (f32[4]{0:T(128)S(1)}, f32[4]{0:T(128)}, u32[]{:S(2)}) copy-start(f32[4]{0:T(128)} %param.27) | copy-start | bytes 52
  0.7 25.6 %copy-start.16 = (f32[1024,128]{1,0:T(8,128)S(1)}, f32[1024,128]{1,0:T(8,128)}, u32[]{:S(2)}) copy-start(f32[1024,128]{1,0:T(8,128)} %param.18) | copy-start | bytes 1572868
  0.7 25.8 %copy-start.18 = (f32[8,12,128]{2,0,1:T(8,128)S(1)}, f32[8,12,128]{2,0,1:T(8,128)}, u32[]{:S(2)}) copy-start(f32[8,12,128]{2,0,1:T(8,128)} %param.25) | copy-start | bytes 147460
  11.1 40.3 %all-to-all-start = ((f32[16,64,1]{1,2,0:T(1,128)}), f32[16,64,1]{1,2,0:T(1,128)S(1)}, u32[]{:S(2)}, u32[]{:S(2)}) async-start(f32[16,64,1]{1,2,0:T(1,128)} %bitcast.20), calls=%async_computation | async-start | bytes 16384 | tf_op jit(solution)/shard_map/all_to_all | solution.py:154
  30.4 13.4 %copy-start.26 = (f32[4]{0:T(128)S(1)}, f32[4]{0:T(128)}, u32[]{:S(2)}) copy-start(f32[4]{0:T(128)} %param.28) | copy-start | bytes 52
  43.8 4.7 %copy-start.2 = (f32[1024,128]{0,1:T(8,128)S(1)}, f32[1024,128]{0,1:T(8,128)}, u32[]{:S(2)}) copy-start(f32[1024,128]{0,1:T(8,128)} %copy-done.1) | copy-start | bytes 1572868
  43.8 4.7 %copy-start.4 = (f32[1024,128]{0,1:T(8,128)S(1)}, f32[1024,128]{0,1:T(8,128)}, u32[]{:S(2)}) copy-start(f32[1024,128]{0,1:T(8,128)} %copy-done.3) | copy-start | bytes 1572868
  43.8 4.7 %copy-start.6 = (f32[1024,128]{0,1:T(8,128)S(1)}, f32[1024,128]{0,1:T(8,128)}, u32[]{:S(2)}) copy-start(f32[1024,128]{0,1:T(8,128)} %copy-done.5) | copy-start | bytes 1572868
  43.8 4.7 %copy-start.8 = (f32[1024,128]{0,1:T(8,128)S(1)}, f32[1024,128]{0,1:T(8,128)}, u32[]{:S(2)}) copy-start(f32[1024,128]{0,1:T(8,128)} %copy-done.7) | copy-start | bytes 1572868
  43.9 4.7 %copy-start.14 = (f32[1024,128]{0,1:T(8,128)S(1)}, f32[1024,128]{0,1:T(8,128)}, u32[]{:S(2)}) copy-start(f32[1024,128]{0,1:T(8,128)} %fusion.46) | copy-start | bytes 1572868
  43.9 4.7 %copy-start.15 = (f32[1024,128]{0,1:T(8,128)S(1)}, f32[1024,128]{0,1:T(8,128)}, u32[]{:S(2)}) copy-start(f32[1024,128]{0,1:T(8,128)} %copy.72) | copy-start | bytes 1572868
  51.4 19.3 %all-to-all-start.2 = ((f32[32,1,512]{2,1,0:T(1,128)}), f32[32,1,512]{2,1,0:T(1,128)S(1)}, u32[]{:S(2)}, u32[]{:S(2)}) async-start(f32[32,1,512]{2,1,0:T(1,128)} %reshape.149), calls=%async_computation.2 | async-start | bytes 131072 | tf_op jit(solution)/shard_map/all_to_all | solution.py:21
  63.0 18.9 %copy-start.23 = (f32[128]{0:T(128)S(1)}, f32[128]{0:T(128)}, u32[]{:S(2)}) copy-start(f32[128]{0:T(128)} %param.30) | copy-start | bytes 1540
  70.7 37.6 %all-to-all-start.1 = ((f32[16,64,256]{2,1,0:T(8,128)}), f32[16,64,256]{2,1,0:T(8,128)S(1)}, u32[]{:S(2)}, u32[]{:S(2)}) async-start(f32[16,64,256]{2,1,0:T(8,128)} %bitcast.22), calls=%async_computation.1 | async-start | bytes 2097152 | tf_op jit(solution)/shard_map/all_to_all | solution.py:153
  109.3 2.7 %copy-start.22 = (f32[8]{0:T(128)S(1)}, f32[8]{0:T(128)}, u32[]{:S(2)}) copy-start(f32[8]{0:T(128)} %param.29) | copy-start | bytes 100
  113.0 73.4 %copy-start.12 = (f32[1024,128]{0,1:T(8,128)S(1)}, f32[1024,128]{0,1:T(8,128)}, u32[]{:S(2)}) copy-start(f32[1024,128]{0,1:T(8,128)} %copy-done.11) | copy-start | bytes 1572868
  113.0 74.4 %copy-start.10 = (f32[1024,128]{0,1:T(8,128)S(1)}, f32[1024,128]{0,1:T(8,128)}, u32[]{:S(2)}) copy-start(f32[1024,128]{0,1:T(8,128)} %copy-done.9) | copy-start | bytes 1572868
  113.0 76.0 %copy-start.13 = (f32[1024,128]{0,1:T(8,128)S(1)}, f32[1024,128]{0,1:T(8,128)}, u32[]{:S(2)}) copy-start(f32[1024,128]{0,1:T(8,128)} %get-tuple-element.148) | copy-start | bytes 1572868
  181.3 19.3 %copy-start.17 = (f32[32,128]{1,0:T(8,128)}, f32[32,128]{1,0:T(8,128)S(1)}, u32[]{:S(2)}) copy-start(f32[32,128]{1,0:T(8,128)S(1)} %copy.82) | copy-start | bytes 49156
  182.0 15.7 %all-to-all-start.3 = ((f32[16,32,128]{2,1,0:T(8,128)}), f32[16,32,128]{2,1,0:T(8,128)S(1)}, u32[]{:S(2)}, u32[]{:S(2)}) async-start(f32[16,32,128]{2,1,0:T(8,128)} %broadcast_in_dim.68), calls=%async_computation.3 | async-start | bytes 524288 | tf_op jit(solution)/shard_map/all_to_all | solution.py:21
  (7 other events, 6.8 us)
where the time goes:
time: 205 us; the launch traced here: 202 us
  matrix products  81.6 us (40%)
  starting transfers between devices  39.6 us (19%)
  local copies, waits for them, and re-layouts  34.1 us (17%)
  waiting for transfers between devices  34.1 us (17%)
  other arithmetic  10 us (5%)
    dot_general x8, matrix products, valuation_batch(): return jnp.dot(weights, payoff, precision=HIGHEST)  37.9 us
    dot_general x8, matrix products, valuation_batch(): lax.dot_general(flat_paths, load_rows, (((0,), (0,)), ((), ())), precisio...  27.7 us
    all_to_all x1, waiting for transfers between devices, body(): lax.all_to_all(payload, 'proj', split_axis=0, concat_axis=0, tiled=True)  23.8 us
    unnamed x66, local copies, waits for them, and re-layouts  16.1 us
    all_to_all x2, starting transfers between devices, sent_to_all(): return lax.all_to_all(copies, axis, split_axis=0, concat_axis=0, tiled=True)  14.3 us
    all_to_all x1, starting transfers between devices, body(): lax.all_to_all(labels, 'proj', split_axis=0, concat_axis=0, tiled=True)  14.2 us
    dot_general x12, matrix products, project(): jnp.dot(mix_rows, returns[:, month_step, :], precision=HIGHEST, preferred...  11.2 us
    all_to_all x1, starting transfers between devices, body(): lax.all_to_all(payload, 'proj', split_axis=0, concat_axis=0, tiled=True)  11.1 us
  transfers between devices with their start and end apart: 4, of which 3 were waited for; matrix products, arithmetic and copies ran while one was open for 17% of the time, Pallas kernels for 0%

commit v1 on v0

v1 whole, which is shorter than its diff:
```python
import functools

import jax
import jax.numpy as jnp
from jax import lax
from jax.experimental import pallas as pl
from jax.experimental.pallas import tpu as pltpu
from jax.sharding import PartitionSpec as P

F32, BF16 = jnp.float32, jnp.bfloat16
MESH = pl.DeviceIdType.MESH
LOG2E = 1.4426950408889634

PLANES, PLANE = 2, 8
RING_Y, RUN_Z = 8, 4
SHARE, BLOCK = 64, 32
ROWS = SHARE + BLOCK + 8
CHUNKS, CHUNK = 4, 8
PART = CHUNK * 8 + CHUNK
KDIM = 32


def split2(x):
    hi = x.astype(BF16).astype(F32)
    return hi, x - hi


def split3(x):
    hi, rest = split2(x)
    mid, lo = split2(rest)
    return hi, mid, lo


def matmul(a, b):
    return jnp.dot(a, b, preferred_element_type=F32)


def rows_of(pieces, lanes):
    row = lax.broadcasted_iota(jnp.int32, (8, lanes), 0)
    out = jnp.zeros((8, lanes), F32)
    for i, piece in enumerate(pieces):
        out = jnp.where(row == i, piece, out)
    return out


def project_kernel(
    blocks,
    fund, force, base, lapse, coh, prod, gtype, ret, mix, fee, roll, table, year,
    fund_o, force_o, base_o, ws_o, ss_o, ri_o,
    fb, ib, bb, lb, wsb, ssb, lm, rm, sem_in, sem_out,
):
    points = fb.shape[0]
    size = points // blocks
    months = ret.shape[0]

    def copies_in(i):
        at = pl.ds(i * size, size)
        return [
            pltpu.make_async_copy(src.at[at], dst.at[at], sem_in.at[i, n])
            for n, (src, dst) in enumerate(((fund, fb), (force, ib), (base, bb), (lapse, lb)))
        ]

    def copies_out(i):
        at = pl.ds(i * size, size)
        return [
            pltpu.make_async_copy(src.at[at], dst.at[at], sem_out.at[i, n])
            for n, (src, dst) in enumerate(
                ((fb, fund_o), (ib, force_o), (bb, base_o), (wsb, ws_o), (ssb, ss_o))
            )
        ]

    for i in range(blocks):
        for c in copies_in(i):
            c.start()

    products = mix.shape[1]
    m = mix[...]
    mix_norm = m / jnp.sum(m, axis=0, keepdims=True)
    prod_row = prod[...]
    hot = jnp.where(
        lax.broadcasted_iota(jnp.int32, (products, points), 0) == prod_row, 1.0, 0.0
    )
    mix_rows = jnp.dot(
        mix_norm, hot, precision=lax.Precision.HIGHEST, preferred_element_type=F32
    )
    g = gtype[...]
    fee_row, roll_row = jnp.zeros(g.shape, F32), jnp.zeros(g.shape, F32)
    for k in range(fee.shape[0]):
        fee_row = jnp.where(g == k, fee[k], fee_row)
        roll_row = jnp.where(g == k, roll[k], roll_row)
    grow = 1.0 + roll_row / 12.0
    kappa = (1.0 - fee_row) / grow
    g2 = grow * grow
    g4 = g2 * g2
    grow_year = g4 * g4 * g4
    a_hi, a_lo = split2(mix_rows * kappa)
    extra = rows_of([*split3(kappa), *split3(grow_year)], points)
    lhs = jnp.concatenate([a_hi, a_hi, a_lo, extra], axis=0)
    lm[...] = lhs.T.astype(BF16)
    row8 = lax.broadcasted_iota(jnp.int32, (8, 128), 0)
    ones = jnp.where(row8 < 3, 1.0, 0.0)
    for t in range(months):
        r_hi, r_lo = split2(ret[t])
        tile = jnp.concatenate([r_hi, r_lo, r_hi, ones], axis=0)
        rm[:, t * 128 : (t + 1) * 128] = tile.astype(BF16)
    last = jnp.where((row8 >= 3) & (row8 < 6), 1.0, 0.0)
    zero = jnp.zeros((8, 128), F32)
    rm[:, months * 128 : (months + 1) * 128] = jnp.concatenate(
        [zero, zero, zero, last], axis=0
    ).astype(BF16)

    owners = points // SHARE
    coh_row = coh[...]
    owner_row = lax.div(coh_row, BLOCK)
    owner_iota = lax.broadcasted_iota(jnp.int32, (owners, points), 0)
    owner_hot = jnp.where(owner_iota == owner_row, 1.0, 0.0)
    before = jnp.where(
        lax.broadcasted_iota(jnp.int32, (128, 128), 0)
        < lax.broadcasted_iota(jnp.int32, (128, 128), 1),
        1.0, 0.0,
    ).astype(BF16)
    offset = lax.broadcasted_iota(jnp.int32, (owners, 1), 0).astype(F32) * float(SHARE)
    places = []
    for b in range(points // 128):
        part = owner_hot[:, b * 128 : (b + 1) * 128]
        rank = matmul(part.astype(BF16), before) + offset
        places.append(jnp.sum(part * rank, axis=0, keepdims=True))
        offset = offset + jnp.sum(part, axis=1, keepdims=True)
    place = jnp.concatenate(places, axis=1)
    lapses = jnp.dot(
        table[...], hot, precision=lax.Precision.HIGHEST, preferred_element_type=F32
    )
    picked = lax.broadcasted_iota(jnp.int32, lapses.shape, 0) == year[0]
    base_lapse = jnp.sum(jnp.where(picked, lapses, 0.0), axis=0, keepdims=True)
    local = coh_row - owner_row * BLOCK
    ri_o[...] = rows_of(
        [place, coh_row.astype(F32), base_lapse, local.astype(F32), prod_row.astype(F32)], points
    )

    step = 128
    for i in range(blocks):
        for c in copies_in(i):
            c.wait()
        for j in range(size // step):
            at = pl.ds(i * size + j * step, step)
            left = lm[at, :]
            f, b = fb[at, :], bb[at, :]
            for t in range(0, months, 2):
                growth = matmul(left, rm[:, t * 128 : (t + 2) * 128])
                f = f * growth[:, :128]
                b = jnp.maximum(b, f)
                f = f * growth[:, 128:]
                b = jnp.maximum(b, f)
            scale = matmul(left, rm[:, months * 128 : (months + 1) * 128])
            f, b = f * scale, b * scale
            s = 1.0 - lb[at, :] / 12.0
            s2 = s * s
            s4 = s2 * s2
            n = ib[at, :] * (s4 * s4 * s4)
            fb[at, :], bb[at, :], ib[at, :] = f, b, n
            w_hi, w_lo = split2(n * f)
            wsb[at, 0:128], wsb[at, 128:256] = w_hi.astype(BF16), w_lo.astype(BF16)
            s_hi, s_lo = split2(n * b)
            ssb[at, 0:128], ssb[at, 128:256] = s_hi.astype(BF16), s_lo.astype(BF16)
        for c in copies_out(i):
            c.start()
    for i in range(blocks):
        for c in copies_out(i):
            c.wait()


def value_kernel(
    ws_h, ss_h, ri, sh, sigma, vol, mix,
    lapse_o, cost_o,
    wsv, ssv, hot, sb, rb, wmat, mh, ml, zs, zr, own,
    p1s, p1r, p2s, p2r, lhs, lfv, cb, pick, brow, out,
    sem_in, sem_out, x_s, x_r, z_s, z_r, a_s, a_r, y_s, y_r, c_s, c_r, o_s, o_r, f_s, f_r,
):
    points = ri.shape[1]
    me, col = lax.axis_index("proj"), lax.axis_index("scen")
    h, u = lax.div(me, PLANE), lax.rem(me, PLANE)
    y, zl = lax.div(col, RUN_Z), lax.rem(col, RUN_Z)
    across = (1 - h) * PLANE + u
    peers = [h * PLANE + lax.rem(u + r, PLANE) for r in range(1, PLANE)]
    z_peers = [y * RUN_Z + lax.rem(zl + r, RUN_Z) for r in range(1, RUN_Z)]
    y_peers = [lax.rem(y + r, RING_Y) * RUN_Z + zl for r in range(1, RING_Y)]

    barrier = pltpu.get_barrier_semaphore()
    for p in [*peers, across]:
        pl.semaphore_signal(barrier, inc=1, device_id={"proj": p}, device_id_type=MESH)
    for p in [*z_peers, *y_peers]:
        pl.semaphore_signal(barrier, inc=1, device_id={"scen": p}, device_id_type=MESH)

    ins = [
        pltpu.make_async_copy(ws_h, wsv, sem_in.at[0]),
        pltpu.make_async_copy(ss_h, ssv, sem_in.at[1]),
    ]
    for c in ins:
        c.start()

    lane = lax.broadcasted_iota(jnp.int32, (8, 128), 1)
    place, coh_row = ri[0:1, :], ri[1:2, :]
    row16 = lax.broadcasted_iota(jnp.int32, (16, points), 0)

    first = sh[:, 0, :]
    paths = jnp.concatenate([first, first + sh[:, 1, :]], axis=0)
    spread = jnp.concatenate([paths] * RUN_Z, axis=1)
    lane16 = lax.broadcasted_iota(jnp.int32, (16, 128), 1)
    p1s[...] = jnp.where(lax.div(lane16, 128 // RUN_Z) == zl, spread, 0.0)

    m = mix[...]
    mix_norm = m / jnp.sum(m, axis=0, keepdims=True)
    mix_pair = jnp.concatenate(split2(mix_norm), axis=0).astype(BF16)
    labels = rows_of([ri[3:4, :], ri[4:5, :]], points).astype(BF16)

    def to_proj(src, dst, s, r, p):
        return pltpu.make_async_remote_copy(
            src_ref=src, dst_ref=dst, send_sem=s, recv_sem=r,
            device_id={"proj": p}, device_id_type=MESH,
        )

    def to_scen(src, dst, s, r, p):
        return pltpu.make_async_remote_copy(
            src_ref=src, dst_ref=dst, send_sem=s, recv_sem=r,
            device_id={"scen": p}, device_id_type=MESH,
        )

    def one_hots(plane):
        def values(i, _):
            want = (row16 + (plane * (PLANE * SHARE) + i * 16)).astype(F32)
            hot[pl.ds(pl.multiple_of(i * 16, 16), 16), :] = jnp.where(
                place == want, 1.0, 0.0
            ).astype(BF16)
            return 0

        def sums(i, _):
            want = (row16 + (plane * (PLANE * BLOCK) + i * 16)).astype(F32)
            hot[pl.ds(pl.multiple_of(PLANE * SHARE + i * 16, 16), 16), :] = jnp.where(
                coh_row == want, 1.0, 0.0
            ).astype(BF16)
            return 0

        lax.fori_loop(0, PLANE * SHARE // 16, values, 0)
        lax.fori_loop(0, PLANE * BLOCK // 16, sums, 0)

    def pack(k):
        got = matmul(hot[0 : PLANE * SHARE, :], wsv[...])
        for b in range(PLANE):
            part = got[b * SHARE : (b + 1) * SHARE]
            sb[k, b, 0:SHARE, :] = part[:, :128] + part[:, 128:]
        got = matmul(hot[PLANE * SHARE :, :], ssv[...])
        for b in range(PLANE):
            part = got[b * BLOCK : (b + 1) * BLOCK]
            sb[k, b, SHARE : SHARE + BLOCK, :] = part[:, :128] + part[:, 128:]
        lab = lax.dot_general(
            labels, hot[0 : PLANE * SHARE, :], (((1,), (1,)), ((), ())),
            preferred_element_type=F32,
        )
        for i in range(PLANE // 2):
            x = lab[:, i * 128 : (i + 1) * 128]
            back = pltpu.roll(x, 64, 1)
            sb[k, 2 * i, SHARE + BLOCK :, :] = jnp.where(lane < 64, x, back)
            sb[k, 2 * i + 1, SHARE + BLOCK :, :] = jnp.where(lane < 64, back, x)

    def send(k):
        sent = []
        for r in range(1, PLANE):
            sent.append(
                to_proj(
                    sb.at[k, lax.rem(u + r, PLANE)], rb.at[k, r - 1],
                    x_s.at[k, r - 1], x_r.at[k, r - 1], peers[r - 1],
                )
            )
            sent[-1].start()
        return sent

    def partial(k, dst):
        labs = []
        total = sb[k, u, SHARE : SHARE + BLOCK, :]
        for n in range(PLANE):
            mine = n == PLANE - 1
            part = sb[k, u, 0:SHARE, :] if mine else rb[k, n, 0:SHARE, :]
            hi, lo = split2(part)
            wmat[n * SHARE : (n + 1) * SHARE, 0:128] = hi.astype(BF16)
            wmat[n * SHARE : (n + 1) * SHARE, 128:256] = lo.astype(BF16)
            labs.append(sb[k, u, SHARE + BLOCK :, :] if mine else rb[k, n, SHARE + BLOCK :, :])
            if not mine:
                total = total + rb[k, n, SHARE : SHARE + BLOCK, :]
        lab = jnp.concatenate(
            [jnp.where(lane < 64, labs[2 * i], labs[2 * i + 1]) for i in range(PLANE // 2)], axis=1
        )
        arrived = PLANE * SHARE
        here, which = lab[0:1, :], lab[1:2, :]
        prod_hot = jnp.where(
            lax.broadcasted_iota(jnp.int32, (mix.shape[1], arrived), 0).astype(F32) == which,
            1.0, 0.0,
        ).astype(BF16)
        pair = matmul(mix_pair, prod_hot)
        m_hi, m_lo = pair[0:8], pair[8:16]

        def members(i, _):
            even = here == (2 * i).astype(F32)
            odd = here == (2 * i + 1).astype(F32)
            at = pl.ds(pl.multiple_of(i * 16, 16), 16)
            for ref, v in ((mh, m_hi), (ml, m_lo)):
                ref[at, :] = jnp.concatenate(
                    [jnp.where(even, v, 0.0), jnp.where(odd, v, 0.0)], axis=0
                ).astype(BF16)
            return 0

        lax.fori_loop(0, BLOCK // 2, members, 0)
        both = matmul(mh[...], wmat[...])
        sums = both[:, :128] + both[:, 128:] + matmul(ml[...], wmat[:, 0:128])
        for j in range(CHUNKS):
            dst[j, 0 : CHUNK * 8, :] = sums[j * CHUNK * 8 : (j + 1) * CHUNK * 8]
            dst[j, CHUNK * 8 :, :] = total[j * CHUNK : (j + 1) * CHUNK]

    one_hots(1 - h)
    for c in ins:
        c.wait()
    pack(0)
    pl.semaphore_wait(barrier, len(peers) + 1 + len(z_peers) + len(y_peers))
    x_sent = [send(0)]
    a_sent = [
        to_scen(p1s, p1r.at[r], a_s.at[r], a_r.at[r], z_peers[r]) for r in range(RUN_Z - 1)
    ]
    for c in a_sent:
        c.start()
    one_hots(h)
    pack(1)
    x_sent.append(send(1))

    for c in a_sent:
        c.wait_recv()
    p2s[...] = p1s[...] + p1r[0] + p1r[1] + p1r[2]
    y_sent = [
        to_scen(p2s, p2r.at[r], y_s.at[r], y_r.at[r], y_peers[r]) for r in range(RING_Y - 1)
    ]
    for c in y_sent:
        c.start()

    cols = ri[...].T
    brow[...] = jnp.broadcast_to(cols[:, 2:3], brow.shape)
    coh_col = cols[:, 1:2]
    for n in range(pick.shape[1] // 128):
        cohorts = (lax.broadcasted_iota(jnp.int32, (points, 128), 1) + n * 128).astype(F32)
        pick[:, n * 128 : (n + 1) * 128] = jnp.where(coh_col == cohorts, 1.0, 0.0).astype(BF16)

    for c in x_sent[0]:
        c.wait_recv()
    partial(0, zs)
    z_sent = [
        to_proj(zs.at[j], zr.at[j], z_s.at[j], z_r.at[j], across) for j in range(CHUNKS)
    ]
    for c in z_sent:
        c.start()

    for c in y_sent:
        c.wait_recv()
    row8 = lax.broadcasted_iota(jnp.int32, (8, 128), 0)
    for n in range(RING_Y):
        tile = p2s[...] if n == RING_Y - 1 else p2r[n]
        for k in range(2):
            hi, lo = split2(tile[k * 8 : (k + 1) * 8])
            years = jnp.where(row8 < 3, float(k + 1), 0.0)
            full = jnp.concatenate([hi, hi, lo, years], axis=0)
            at = (k * RING_Y + n) * 128
            lhs[at : at + 128, :] = full.T.astype(BF16)

    for c in x_sent[1]:
        c.wait_recv()
    partial(1, own)

    trials = RING_Y * 128
    vols = rows_of([vol[f] for f in range(8)], 128)
    sig = sigma[...]
    level = sig * LOG2E
    drift = sig * sig * (-0.5 * LOG2E)
    c_sent = []
    for j in range(CHUNKS):
        z_sent[j].wait_recv()

        def price(i, _):
            tiles, money = [], []
            for e in range(2):
                c = i * 2 + e
                at = pl.ds(pl.multiple_of(c * 8, 8), 8)
                s = own[j, at, :] + zr[j, at, :]
                g = own[j, pl.ds(CHUNK * 8 + c, 1), :] + zr[j, pl.ds(CHUNK * 8 + c, 1), :]
                inv = 1.0 / jnp.sum(s, axis=0, keepdims=True)
                loads = s * inv * vols
                d = drift * jnp.sum(loads * loads, axis=0, keepdims=True)
                a_hi, a_lo = split2(loads * level)
                tiles.append(
                    jnp.concatenate([a_hi, a_lo, a_hi, rows_of(split3(d), 128)], axis=0)
                )
                money.append(g * inv)
            right = jnp.concatenate(tiles, axis=1).astype(BF16)
            strike = jnp.concatenate(money, axis=1)
            cost = jnp.zeros((1, 256), F32)
            for k in range(2):
                acc = jnp.zeros((8, 256), F32)
                for b in range(0, trials, 256):
                    at = k * trials + b
                    x = matmul(lhs[at : at + 256, :], right)
                    pay = jnp.maximum(strike - jnp.exp2(x), 0.0)
                    acc = acc + jnp.sum(pay.reshape(32, 8, 256), axis=0)
                cost = cost + jnp.sum(acc, axis=0, keepdims=True) * (0.96 ** (k + 1) / trials)
            factor = 0.3 + 2.0 / (1.0 + jnp.exp(5.0 * cost - 2.0))
            for e in range(2):
                at = pl.ds(j * CHUNK + i * 2 + e, 1)
                cost_o[at, :] = cost[:, e * 128 : (e + 1) * 128]
                lfv[at, :] = factor[:, e * 128 : (e + 1) * 128]
            return 0

        lax.fori_loop(0, CHUNK // 2, price, 0)
        c_sent.append(
            to_proj(
                lfv.at[pl.ds(j * CHUNK, CHUNK)],
                cb.at[pl.ds(pl.multiple_of(me * BLOCK + j * CHUNK, 8), CHUNK)],
                c_s.at[j], c_r.at[j], across,
            )
        )
        c_sent[-1].start()

    o_sent = [
        to_proj(
            lfv, cb.at[pl.ds(pl.multiple_of(me * BLOCK, 8), BLOCK)],
            o_s.at[r], o_r.at[r], peers[r],
        )
        for r in range(PLANE - 1)
    ]
    for c in o_sent:
        c.start()
    cb[pl.ds(pl.multiple_of(me * BLOCK, 8), BLOCK), :] = lfv[...]
    f_sent = []
    half = BLOCK // 2
    for n in range(2):
        for j in range(n * CHUNKS // 2, (n + 1) * CHUNKS // 2):
            c_sent[j].wait_recv()
        at = pl.ds(pl.multiple_of(across * BLOCK + n * half, 8), half)
        for r in range(PLANE - 1):
            f_sent.append(to_proj(cb.at[at], cb.at[at], f_s.at[n, r], f_r.at[n, r], peers[r]))
            f_sent[-1].start()
    for c in [*o_sent, *f_sent]:
        c.wait_recv()

    hi, lo = split2(cb[...])
    factors = jnp.concatenate([hi, lo], axis=1).astype(BF16)
    blocks = sem_out.shape[0]
    size = points // blocks
    outs = []
    for i in range(blocks):
        at = pl.ds(i * size, size)
        got = matmul(pick[at, :], factors)
        out[at, :] = (got[:, :128] + got[:, 128:]) * brow[at, :]
        outs.append(pltpu.make_async_copy(out.at[at], lapse_o.at[at], sem_out.at[i]))
        outs[-1].start()
    for c in [*x_sent[0], *x_sent[1], *a_sent, *y_sent, *z_sent, *c_sent, *o_sent, *f_sent]:
        c.wait_send()
    for c in outs:
        c.wait()


def body(
    fund_value, in_force, guarantee_base, lapse_rate, cohort, product, guarantee_type,
    returns, mix_table, fee_table, rollup_table, fund_vol, closing_sigma_figure, shocks,
    base_table, year_index,
):
    points, scens = fund_value.shape
    cohorts = BLOCK * lax.axis_size("proj")
    blocks = 4
    vmem = pl.BlockSpec(memory_space=pltpu.VMEM)
    smem = pl.BlockSpec(memory_space=pltpu.SMEM)
    hbm = pl.BlockSpec(memory_space=pl.ANY)
    dma = pltpu.SemaphoreType.DMA
    full = jax.ShapeDtypeStruct((points, scens), F32)
    pair = jax.ShapeDtypeStruct((points, 2 * scens), BF16)
    months = returns.shape[1]
    fund_next, force_next, base_next, ws, ss, ri = pl.pallas_call(
        functools.partial(project_kernel, blocks),
        out_shape=(full, full, full, pair, pair, jax.ShapeDtypeStruct((8, points), F32)),
        in_specs=[hbm] * 4 + [vmem] * 5 + [smem] * 2 + [vmem, smem],
        out_specs=(hbm,) * 5 + (vmem,),
        scratch_shapes=[
            *[pltpu.VMEM((points, scens), F32)] * 4,
            *[pltpu.VMEM((points, 2 * scens), BF16)] * 2,
            pltpu.VMEM((points, KDIM), BF16),
            pltpu.VMEM((KDIM, (months + 1) * scens), BF16),
            dma((blocks, 4)),
            dma((blocks, 5)),
        ],
    )(
        fund_value, in_force, guarantee_base, lapse_rate,
        cohort.reshape(1, points), product.reshape(1, points), guarantee_type.reshape(1, points),
        returns.transpose(1, 0, 2), mix_table.T, fee_table, rollup_table, base_table, year_index,
    )
    lapse_next, cost = pl.pallas_call(
        value_kernel,
        out_shape=(full, jax.ShapeDtypeStruct((BLOCK, scens), F32)),
        in_specs=[hbm] * 2 + [vmem] * 3 + [smem, vmem],
        out_specs=(hbm, vmem),
        scratch_shapes=[
            *[pltpu.VMEM((points, 2 * scens), BF16)] * 2,
            pltpu.VMEM((PLANE * (SHARE + BLOCK), points), BF16),
            pltpu.VMEM((2, PLANE, ROWS, scens), F32),
            pltpu.VMEM((2, PLANE - 1, ROWS, scens), F32),
            pltpu.VMEM((PLANE * SHARE, 2 * scens), BF16),
            *[pltpu.VMEM((BLOCK * 8, PLANE * SHARE), BF16)] * 2,
            *[pltpu.VMEM((CHUNKS, PART, scens), F32)] * 3,
            pltpu.VMEM((16, 128), F32),
            pltpu.VMEM((RUN_Z - 1, 16, 128), F32),
            pltpu.VMEM((16, 128), F32),
            pltpu.VMEM((RING_Y - 1, 16, 128), F32),
            pltpu.VMEM((2 * RING_Y * 128, KDIM), BF16),
            pltpu.VMEM((BLOCK, scens), F32),
            pltpu.VMEM((cohorts, scens), F32),
            pltpu.VMEM((points, cohorts), BF16),
            pltpu.VMEM((points, scens), F32),
            pltpu.VMEM((points, scens), F32),
            dma((2,)),
            dma((4,)),
            *[dma((2, PLANE - 1))] * 2,
            *[dma((CHUNKS,))] * 2,
            *[dma((RUN_Z - 1,))] * 2,
            *[dma((RING_Y - 1,))] * 2,
            *[dma((CHUNKS,))] * 2,
            *[dma((PLANE - 1,))] * 2,
            *[dma((2, PLANE - 1))] * 2,
        ],
        compiler_params=pltpu.CompilerParams(collective_id=0, has_side_effects=True),
    )(ws, ss, ri, shocks, closing_sigma_figure.reshape(1, scens), fund_vol, mix_table.T)
    return fund_next, force_next, base_next, lapse_next, cost


def solution(mesh):
    wide, row, last = P("proj", "scen"), P("proj"), P(None, None, "scen")
    placed = (
        wide, wide, wide, wide, row, row, row, last,
        P(), P(), P(), P(), P("scen"), last, P(), P(),
    )
    return jax.shard_map(
        body, mesh=mesh, in_specs=placed, out_specs=(wide,) * 5, check_vma=False
    )
```

time: 205 us -> 54.7 us (0.27); the launches traced: 202 us -> 54.3 us
  matrix products: 81.6 us -> 0 us
  Pallas kernels: 0 us -> 50.5 us
  starting transfers between devices: 39.6 us -> 0 us
  waiting for transfers between devices: 34.1 us -> 0 us
  local copies, waits for them, and re-layouts: 34.1 us -> 2.48 us
  other arithmetic: 10 us -> 0 us
    dot_general x34 -> x0, matrix products: 81.6 us -> none  [the longest x8 37.9 us: valuation_batch(): return jnp.dot(weights, payoff, precision=HIGHEST)]
    pallas_call x0 -> x2, Pallas kernels: none -> 50.5 us  [the longest x1 45.3 us: body(): pl.pallas_call(value_kernel, out_shape=(full, jax.ShapeDtypeStruct((BLOCK...]
    all_to_all x4 -> x0, starting transfers between devices: 39.6 us -> none  [the longest x2 14.3 us: sent_to_all(): return lax.all_to_all(copies, axis, split_axis=0, concat_axis=0, tiled=True)]
    all_to_all x4 -> x0, waiting for transfers between devices: 34.1 us -> none  [the longest x1 23.8 us: body(): lax.all_to_all(payload, 'proj', split_axis=0, concat_axis=0, tiled=True)]
    unnamed x66 -> x4, local copies, waits for them, and re-layouts: 16.1 us -> 2.48 us
    gather x4 -> x0, local copies, waits for them, and re-layouts: 12.2 us -> none  [the longest x1 4.66 us: body(): payload = jnp.concatenate([weighted, secured], axis=1)[order]]
    sort x1 -> x0, other arithmetic: 4.37 us -> none  [body(): order = jnp.argsort(owner, stable=True)]
    mul x12 -> x0, other arithmetic: 2.64 us -> none  [the longest x1 1.79 us: body(): secured = force_next * base_next]
  transfers between devices with their start and end apart: 4 -> 0, of which waited for: 3 -> 0; matrix products, arithmetic and copies ran while one was open for 17% -> 0% of each run, Pallas kernels for 0% -> 0%
where the time goes in v1:
time: 54.7 us; the launch traced here: 54.3 us
  Pallas kernels  50.5 us (92%)
  local copies, waits for them, and re-layouts  2.48 us (5%)
  between operations  1.31 us (2%)
    pallas_call x1, Pallas kernels, body(): pl.pallas_call(value_kernel, out_shape=(full, jax.ShapeDtypeStruct((BLOCK...  45.3 us
    pallas_call x1, Pallas kernels, body(): pl.pallas_call(functools.partial(project_kernel, blocks), out_shape=(full...  5.24 us
    unnamed x4, local copies, waits for them, and re-layouts  2.48 us

profile of v1, /device:TPU:1, one launch (start us, length us, event | category | flops | bytes accessed | tf_op | source)
XLA Modules:
  0.0 54.3 jit_solution(9480336420729619965)
XLA Ops:
  1.3 5.2 %shard_map.191 = (f32[1024,128]{1,0:T(8,128)}, f32[1024,128]{1,0:T(8,128)}, f32[1024,128]{1,0:T(8,128)}, bf16[1024,256]{1,0:T(8,128)(2,1)}, bf16[1024,256]{1,0:T(8,128)(2,1)}, /*index=5*/f32[8,1024]{1,0:T(8,128)}) custom-call(f32[1024,128]{1,0:T(8,128)} %fund.1, f32[1024,128]{1,0:T(8,128)} %force.1, f32[1024,128]{1,0:T(8,128)} %base.1, f32[1024,128]{1,0:T(8,128)} %lapse.1, ...), custom_call_target="tpu_custom_call" | custom-call | tf_op jit(solution)/shard_map/pallas_call | solution.py:480
  6.5 45.3 %shard_map.192 = (f32[1024,128]{1,0:T(8,128)}, f32[32,128]{1,0:T(8,128)}) custom-call(bf16[1024,256]{1,0:T(8,128)(2,1)} %get-tuple-element.16.ws_h, bf16[1024,256]{1,0:T(8,128)(2,1)} %get-tuple-element.17.ss_h, f32[8,1024]{1,0:T(8,128)} %get-tuple-element.18.ri, f32[8,2,32]{2,1,0:T(2,128)} %sh.1, f32[1,128]{1,0:T(1,128)} %bitcast.12, f32[8]{0:T(128)} %vol.1, ...), custom_call_target="tpu_custom_call" | custom-call | tf_op jit(solution)/shard_map/pallas_call | solution.py:498
  51.8 0.0 copy-start
  51.9 1.9 %copy.24 = f32[1024,128]{1,0:T(8,128)} copy(f32[1024,128]{1,0:T(8,128)} %get-tuple-element.29) | data formatting | bytes 1048576
  53.7 0.0 copy-done
  53.7 0.6 %copy.25 = f32[32,128]{1,0:T(8,128)} copy(f32[32,128]{1,0:T(8,128)S(1)} %copy-done) | data formatting | bytes 32768
Async XLA Ops:
  51.8 1.9 %copy-start = (f32[32,128]{1,0:T(8,128)S(1)}, f32[32,128]{1,0:T(8,128)}, u32[]{:S(2)}) copy-start(f32[32,128]{1,0:T(8,128)} %get-tuple-element.30) | copy-start | bytes 49156

commit v2 on v1

v2 whole, which is shorter than its diff:
```python
import functools

import jax
import jax.numpy as jnp
from jax import lax
from jax.experimental import pallas as pl
from jax.experimental.pallas import tpu as pltpu
from jax.sharding import PartitionSpec as P

F32, BF16 = jnp.float32, jnp.bfloat16
MESH = pl.DeviceIdType.MESH
LOG2E = 1.4426950408889634

PLANES, PLANE = 2, 8
RING_Y, RUN_Z = 8, 4
SHARE, BLOCK = 64, 32
ROWS = SHARE + BLOCK
CHUNKS, CHUNK = 4, 8
PART = CHUNK * 8 + CHUNK
KDIM = 32


def split2(x):
    hi = x.astype(BF16).astype(F32)
    return hi, x - hi


def split3(x):
    hi, rest = split2(x)
    mid, lo = split2(rest)
    return hi, mid, lo


def matmul(a, b):
    return jnp.dot(a, b, preferred_element_type=F32)


def rows_of(pieces, lanes):
    row = lax.broadcasted_iota(jnp.int32, (8, lanes), 0)
    out = jnp.zeros((8, lanes), F32)
    for i, piece in enumerate(pieces):
        out = jnp.where(row == i, piece, out)
    return out


def main_kernel(
    blocks,
    fund, force, base, lapse, coh_h, prod_h, gtype_h, ret_h, mix_h, table_h, sh_h, sigma_h,
    fee_h, roll_h, vol_h, year,
    fund_o, force_o, base_o, pick, brow, cb, cost_o,
    lb, coh, prod, gtype, ret, mix, table, sh, sigma, fee, roll, vol,
    lm, rm, wsv, ssv, hot, sl, rl, sb, rb, wmat, mh, ml, zs, zr, own,
    p1s, p1r, p2s, p2r, lhs, lfv,
    sem_small, sem_in,
    l_s, l_r, x_s, x_r, z_s, z_r, a_s, a_r, y_s, y_r, c_s, c_r,
):
    points = lb.shape[0]
    size = points // blocks
    months = ret.shape[0]
    me, col = lax.axis_index("proj"), lax.axis_index("scen")
    h, u = lax.div(me, PLANE), lax.rem(me, PLANE)
    y, zl = lax.div(col, RUN_Z), lax.rem(col, RUN_Z)
    across = (1 - h) * PLANE + u
    peers = [h * PLANE + lax.rem(u + r, PLANE) for r in range(1, PLANE)]
    far = [(1 - h) * PLANE + lax.rem(u + r, PLANE) for r in range(1, PLANE)]
    z_peers = [y * RUN_Z + lax.rem(zl + r, RUN_Z) for r in range(1, RUN_Z)]
    y_peers = [lax.rem(y + r, RING_Y) * RUN_Z + zl for r in range(1, RING_Y)]

    barrier = pltpu.get_barrier_semaphore()
    for p in [*far, across, *peers]:
        pl.semaphore_signal(barrier, inc=1, device_id={"proj": p}, device_id_type=MESH)
    for p in [*z_peers, *y_peers]:
        pl.semaphore_signal(barrier, inc=1, device_id={"scen": p}, device_id_type=MESH)

    smalls = [
        pltpu.make_async_copy(src, dst, sem_small.at[n])
        for n, (src, dst) in enumerate((
            (coh_h, coh), (prod_h, prod), (gtype_h, gtype), (mix_h, mix), (fee_h, fee),
            (roll_h, roll), (vol_h, vol), (ret_h, ret), (table_h, table),
            (sh_h, sh), (sigma_h, sigma),
        ))
    ]

    def copies_in(i):
        at = pl.ds(i * size, size)
        return [
            pltpu.make_async_copy(src.at[at], dst.at[at], sem_in.at[i, n])
            for n, (src, dst) in enumerate(
                ((fund, fund_o), (base, base_o), (force, force_o), (lapse, lb))
            )
        ]

    for c in smalls:
        c.start()
    for i in range(blocks):
        for c in copies_in(i):
            c.start()
    for c in smalls:
        c.wait()

    lane = lax.broadcasted_iota(jnp.int32, (8, 128), 1)
    row8 = lax.broadcasted_iota(jnp.int32, (8, 128), 0)
    row16 = lax.broadcasted_iota(jnp.int32, (16, points), 0)

    owners = points // SHARE
    coh_row = coh[...]
    owner_row = lax.div(coh_row, BLOCK)
    owner_iota = lax.broadcasted_iota(jnp.int32, (owners, points), 0)
    owner_hot = jnp.where(owner_iota == owner_row, 1.0, 0.0)
    before = jnp.where(
        lax.broadcasted_iota(jnp.int32, (128, 128), 0)
        < lax.broadcasted_iota(jnp.int32, (128, 128), 1),
        1.0, 0.0,
    ).astype(BF16)
    offset = lax.broadcasted_iota(jnp.int32, (owners, 1), 0).astype(F32) * float(SHARE)
    places = []
    for b in range(points // 128):
        part = owner_hot[:, b * 128 : (b + 1) * 128]
        rank = matmul(part.astype(BF16), before) + offset
        places.append(jnp.sum(part * rank, axis=0, keepdims=True))
        offset = offset + jnp.sum(part, axis=1, keepdims=True)
    place = jnp.concatenate(places, axis=1)
    prod_row = prod[...]
    coh_f = coh_row.astype(F32)
    labels = rows_of(
        [(coh_row - owner_row * BLOCK).astype(F32), prod_row.astype(F32)], points
    ).astype(BF16)

    for k in range(2):
        plane = 1 - h if k == 0 else h

        def values(i, _):
            want = (row16 + (plane * (PLANE * SHARE) + i * 16)).astype(F32)
            hot[k, pl.ds(pl.multiple_of(i * 16, 16), 16), :] = jnp.where(
                place == want, 1.0, 0.0
            ).astype(BF16)
            return 0

        def sums(i, _):
            want = (row16 + (plane * (PLANE * BLOCK) + i * 16)).astype(F32)
            hot[k, pl.ds(pl.multiple_of(PLANE * SHARE + i * 16, 16), 16), :] = jnp.where(
                coh_f == want, 1.0, 0.0
            ).astype(BF16)
            return 0

        lax.fori_loop(0, PLANE * SHARE // 16, values, 0)
        lax.fori_loop(0, PLANE * BLOCK // 16, sums, 0)
        lab = lax.dot_general(
            labels, hot[k, 0 : PLANE * SHARE, :], (((1,), (1,)), ((), ())),
            preferred_element_type=F32,
        )
        for i in range(PLANE // 2):
            x = lab[:, i * 128 : (i + 1) * 128]
            back = pltpu.roll(x, 64, 1)
            sl[k, 2 * i] = jnp.where(lane < 64, x, back)
            sl[k, 2 * i + 1] = jnp.where(lane < 64, back, x)

    products = mix.shape[1]
    m = mix[...]
    mix_norm = m / jnp.sum(m, axis=0, keepdims=True)
    prod_hot = jnp.where(
        lax.broadcasted_iota(jnp.int32, (products, points), 0) == prod_row, 1.0, 0.0
    )
    mix_rows = jnp.dot(
        mix_norm, prod_hot, precision=lax.Precision.HIGHEST, preferred_element_type=F32
    )
    g = gtype[...]
    fee_row, roll_row = jnp.zeros(g.shape, F32), jnp.zeros(g.shape, F32)
    for k in range(fee.shape[0]):
        fee_row = jnp.where(g == k, fee[k], fee_row)
        roll_row = jnp.where(g == k, roll[k], roll_row)
    grow = 1.0 + roll_row / 12.0
    kappa = (1.0 - fee_row) / grow
    g2 = grow * grow
    g4 = g2 * g2
    grow_year = g4 * g4 * g4
    a_hi, a_lo = split2(mix_rows * kappa)
    extra = rows_of([*split3(kappa), *split3(grow_year)], points)
    left_rows = jnp.concatenate([a_hi, a_hi, a_lo, extra], axis=0)
    lm[...] = left_rows.T.astype(BF16)
    ones = jnp.where(row8 < 3, 1.0, 0.0)
    for t in range(months):
        r_hi, r_lo = split2(ret[t])
        tile = jnp.concatenate([r_hi, r_lo, r_hi, ones], axis=0)
        rm[:, t * 128 : (t + 1) * 128] = tile.astype(BF16)
    last = jnp.where((row8 >= 3) & (row8 < 6), 1.0, 0.0)
    zero = jnp.zeros((8, 128), F32)
    rm[:, months * 128 : (months + 1) * 128] = jnp.concatenate(
        [zero, zero, zero, last], axis=0
    ).astype(BF16)

    first = sh[:, 0, :]
    paths = jnp.concatenate([first, first + sh[:, 1, :]], axis=0)
    spread = jnp.concatenate([paths] * RUN_Z, axis=1)
    lane16 = lax.broadcasted_iota(jnp.int32, (16, 128), 1)
    p1s[...] = jnp.where(lax.div(lane16, 128 // RUN_Z) == zl, spread, 0.0)

    def to_proj(src, dst, s, r, p):
        return pltpu.make_async_remote_copy(
            src_ref=src, dst_ref=dst, send_sem=s, recv_sem=r,
            device_id={"proj": p}, device_id_type=MESH,
        )

    def to_scen(src, dst, s, r, p):
        return pltpu.make_async_remote_copy(
            src_ref=src, dst_ref=dst, send_sem=s, recv_sem=r,
            device_id={"scen": p}, device_id_type=MESH,
        )

    pl.semaphore_wait(barrier, 2 * PLANE - 1 + len(z_peers) + len(y_peers))
    l_sent = [[], []]
    for k in range(2):
        for r in range(1, PLANE):
            l_sent[k].append(
                to_proj(
                    sl.at[k, lax.rem(u + r, PLANE)], rl.at[k, r - 1],
                    l_s.at[k, r - 1], l_r.at[k, r - 1], peers[r - 1],
                )
            )
            l_sent[k][-1].start()
    a_sent = [
        to_scen(p1s, p1r.at[r], a_s.at[r], a_r.at[r], z_peers[r]) for r in range(RUN_Z - 1)
    ]
    for c in a_sent:
        c.start()

    step = 128
    for i in range(blocks):
        for c in copies_in(i):
            c.wait()
        for j in range(size // step):
            at = pl.ds(i * size + j * step, step)
            left = lm[at, :]
            f, b = fund_o[at, :], base_o[at, :]
            for t in range(0, months, 2):
                growth = matmul(left, rm[:, t * 128 : (t + 2) * 128])
                f = f * growth[:, :128]
                b = jnp.maximum(b, f)
                f = f * growth[:, 128:]
                b = jnp.maximum(b, f)
            scale = matmul(left, rm[:, months * 128 : (months + 1) * 128])
            f, b = f * scale, b * scale
            s = 1.0 - lb[at, :] / 12.0
            s2 = s * s
            s4 = s2 * s2
            n = force_o[at, :] * (s4 * s4 * s4)
            fund_o[at, :], base_o[at, :], force_o[at, :] = f, b, n
            w_hi, w_lo = split2(n * f)
            wsv[at, 0:128], wsv[at, 128:256] = w_hi.astype(BF16), w_lo.astype(BF16)
            s_hi, s_lo = split2(n * b)
            ssv[at, 0:128], ssv[at, 128:256] = s_hi.astype(BF16), s_lo.astype(BF16)

    x_sent = [[], []]
    for k in range(2):
        got = matmul(hot[k, 0 : PLANE * SHARE, :], wsv[...])
        for b in range(PLANE):
            part = got[b * SHARE : (b + 1) * SHARE]
            sb[k, b, 0:SHARE, :] = part[:, :128] + part[:, 128:]
        got = matmul(hot[k, PLANE * SHARE :, :], ssv[...])
        for b in range(PLANE):
            part = got[b * BLOCK : (b + 1) * BLOCK]
            sb[k, b, SHARE:, :] = part[:, :128] + part[:, 128:]
        for r in range(1, PLANE):
            x_sent[k].append(
                to_proj(
                    sb.at[k, lax.rem(u + r, PLANE)], rb.at[k, r - 1],
                    x_s.at[k, r - 1], x_r.at[k, r - 1], peers[r - 1],
                )
            )
            x_sent[k][-1].start()

    for c in a_sent:
        c.wait_recv()
    p2s[...] = p1s[...] + p1r[0] + p1r[1] + p1r[2]
    y_sent = [
        to_scen(p2s, p2r.at[r], y_s.at[r], y_r.at[r], y_peers[r]) for r in range(RING_Y - 1)
    ]
    for c in y_sent:
        c.start()

    mix_pair = jnp.concatenate(split2(mix_norm), axis=0).astype(BF16)
    for k in range(2):
        for c in l_sent[k]:
            c.wait_recv()
        labs = [rl[k, n] for n in range(PLANE - 1)] + [sl[k, u]]
        lab = jnp.concatenate(
            [jnp.where(lane < 64, labs[2 * i], labs[2 * i + 1]) for i in range(PLANE // 2)], axis=1
        )
        here, which = lab[0:1, :], lab[1:2, :]
        arrived_hot = jnp.where(
            lax.broadcasted_iota(jnp.int32, (products, PLANE * SHARE), 0).astype(F32) == which,
            1.0, 0.0,
        ).astype(BF16)
        pair = matmul(mix_pair, arrived_hot)
        m_hi, m_lo = pair[0:8], pair[8:16]

        def members(i, _):
            even = here == (2 * i).astype(F32)
            odd = here == (2 * i + 1).astype(F32)
            at = pl.ds(pl.multiple_of(i * 16, 16), 16)
            for ref, v in ((mh, m_hi), (ml, m_lo)):
                ref[k, at, :] = jnp.concatenate(
                    [jnp.where(even, v, 0.0), jnp.where(odd, v, 0.0)], axis=0
                ).astype(BF16)
            return 0

        lax.fori_loop(0, BLOCK // 2, members, 0)

    def partial(k, dst):
        for c in x_sent[k]:
            c.wait_recv()
        total = sb[k, u, SHARE:, :]
        for n in range(PLANE):
            mine = n == PLANE - 1
            hi, lo = split2(sb[k, u, 0:SHARE, :] if mine else rb[k, n, 0:SHARE, :])
            wmat[n * SHARE : (n + 1) * SHARE, 0:128] = hi.astype(BF16)
            wmat[n * SHARE : (n + 1) * SHARE, 128:256] = lo.astype(BF16)
            if not mine:
                total = total + rb[k, n, SHARE:, :]
        both = matmul(mh[k], wmat[...])
        sums = both[:, :128] + both[:, 128:] + matmul(ml[k], wmat[:, 0:128])
        for j in range(CHUNKS):
            dst[j, 0 : CHUNK * 8, :] = sums[j * CHUNK * 8 : (j + 1) * CHUNK * 8]
            dst[j, CHUNK * 8 :, :] = total[j * CHUNK : (j + 1) * CHUNK]

    partial(0, zs)
    z_sent = [
        to_proj(zs.at[j], zr.at[j], z_s.at[j], z_r.at[j], across) for j in range(CHUNKS)
    ]
    for c in z_sent:
        c.start()

    lapses = jnp.dot(
        table[...], prod_hot, precision=lax.Precision.HIGHEST, preferred_element_type=F32
    )
    picked = lax.broadcasted_iota(jnp.int32, lapses.shape, 0) == year[0]
    base_lapse = jnp.sum(jnp.where(picked, lapses, 0.0), axis=0, keepdims=True)
    cols = rows_of([coh_f, base_lapse], points).T
    brow[...] = jnp.broadcast_to(cols[:, 1:2], brow.shape)
    coh_col = cols[:, 0:1]
    for n in range(pick.shape[1] // 128):
        cohorts = (lax.broadcasted_iota(jnp.int32, (points, 128), 1) + n * 128).astype(F32)
        pick[:, n * 128 : (n + 1) * 128] = jnp.where(coh_col == cohorts, 1.0, 0.0).astype(BF16)

    for c in y_sent:
        c.wait_recv()
    for n in range(RING_Y):
        tile = p2s[...] if n == RING_Y - 1 else p2r[n]
        for k in range(2):
            hi, lo = split2(tile[k * 8 : (k + 1) * 8])
            years = jnp.where(row8 < 3, float(k + 1), 0.0)
            full = jnp.concatenate([hi, hi, lo, years], axis=0)
            at = (k * RING_Y + n) * 128
            lhs[at : at + 128, :] = full.T.astype(BF16)

    partial(1, own)

    trials = RING_Y * 128
    vols = rows_of([vol[f] for f in range(8)], 128)
    sig = sigma[...]
    level = sig * LOG2E
    drift = sig * sig * (-0.5 * LOG2E)
    c_sent = []
    for j in range(CHUNKS):
        z_sent[j].wait_recv()

        def price(i, _):
            tiles, money = [], []
            for e in range(2):
                c = i * 2 + e
                at = pl.ds(pl.multiple_of(c * 8, 8), 8)
                s = own[j, at, :] + zr[j, at, :]
                g = own[j, pl.ds(CHUNK * 8 + c, 1), :] + zr[j, pl.ds(CHUNK * 8 + c, 1), :]
                inv = 1.0 / jnp.sum(s, axis=0, keepdims=True)
                loads = s * inv * vols
                d = drift * jnp.sum(loads * loads, axis=0, keepdims=True)
                a_hi, a_lo = split2(loads * level)
                tiles.append(
                    jnp.concatenate([a_hi, a_lo, a_hi, rows_of(split3(d), 128)], axis=0)
                )
                money.append(g * inv)
            right = jnp.concatenate(tiles, axis=1).astype(BF16)
            strike = jnp.concatenate(money, axis=1)
            cost = jnp.zeros((1, 256), F32)
            for k in range(2):
                acc = jnp.zeros((8, 256), F32)
                for b in range(0, trials, 256):
                    at = k * trials + b
                    x = matmul(lhs[at : at + 256, :], right)
                    pay = jnp.maximum(strike - jnp.exp2(x), 0.0)
                    acc = acc + jnp.sum(pay.reshape(32, 8, 256), axis=0)
                cost = cost + jnp.sum(acc, axis=0, keepdims=True) * (0.96 ** (k + 1) / trials)
            factor = 0.3 + 2.0 / (1.0 + jnp.exp(5.0 * cost - 2.0))
            for e in range(2):
                at = pl.ds(j * CHUNK + i * 2 + e, 1)
                cost_o[at, :] = cost[:, e * 128 : (e + 1) * 128]
                lfv[at, :] = factor[:, e * 128 : (e + 1) * 128]
            return 0

        lax.fori_loop(0, CHUNK // 2, price, 0)
        for n, p in enumerate([*far, across, *peers]):
            c_sent.append(
                to_proj(
                    lfv.at[pl.ds(j * CHUNK, CHUNK)],
                    cb.at[pl.ds(pl.multiple_of(me * BLOCK + j * CHUNK, 8), CHUNK)],
                    c_s.at[j, n], c_r.at[j, n], p,
                )
            )
            c_sent[-1].start()

    cb[pl.ds(pl.multiple_of(me * BLOCK, 8), BLOCK), :] = lfv[...]
    for c in [*l_sent[0], *l_sent[1], *x_sent[0], *x_sent[1], *a_sent, *y_sent, *z_sent]:
        c.wait_send()
    for c in c_sent:
        c.wait_send()
    for c in c_sent:
        c.wait_recv()


def last_kernel(
    fund, force, base, pick, brow, cb, cost,
    fund_o, force_o, base_o, lapse_o, cost_o,
    out, sem, sem_out,
):
    outs = [
        pltpu.make_async_copy(src, dst, sem.at[n])
        for n, (src, dst) in enumerate(
            ((fund, fund_o), (force, force_o), (base, base_o), (cost, cost_o))
        )
    ]
    for c in outs:
        c.start()
    points = out.shape[0]
    factors = jnp.concatenate(split2(cb[...]), axis=1).astype(BF16)
    blocks = sem_out.shape[0]
    size = points // blocks
    for i in range(blocks):
        at = pl.ds(i * size, size)
        got = matmul(pick[at, :], factors)
        out[at, :] = (got[:, :128] + got[:, 128:]) * brow[at, :]
        outs.append(pltpu.make_async_copy(out.at[at], lapse_o.at[at], sem_out.at[i]))
        outs[-1].start()
    for c in outs:
        c.wait()


def body(
    fund_value, in_force, guarantee_base, lapse_rate, cohort, product, guarantee_type,
    returns, mix_table, fee_table, rollup_table, fund_vol, closing_sigma_figure, shocks,
    base_table, year_index,
):
    points, scens = fund_value.shape
    cohorts = BLOCK * lax.axis_size("proj")
    blocks = 4
    vmem = pl.BlockSpec(memory_space=pltpu.VMEM)
    hbm = pl.BlockSpec(memory_space=pl.ANY)
    dma = pltpu.SemaphoreType.DMA
    full = jax.ShapeDtypeStruct((points, scens), F32)
    own = jax.ShapeDtypeStruct((BLOCK, scens), F32)
    months = returns.shape[1]
    ints = pltpu.VMEM((1, points), jnp.int32)
    args = [
        fund_value, in_force, guarantee_base, lapse_rate,
        cohort.reshape(1, points), product.reshape(1, points), guarantee_type.reshape(1, points),
        returns.transpose(1, 0, 2), mix_table.T, base_table, shocks,
        closing_sigma_figure.reshape(1, scens), fee_table, rollup_table, fund_vol,
    ]
    args = [pltpu.with_memory_space_constraint(a, pltpu.HBM) for a in args]
    middle = pl.pallas_call(
        functools.partial(main_kernel, blocks),
        out_shape=(
            full, full, full,
            jax.ShapeDtypeStruct((points, cohorts), BF16),
            full,
            jax.ShapeDtypeStruct((cohorts, scens), F32),
            own,
        ),
        in_specs=[hbm] * 15 + [pl.BlockSpec(memory_space=pltpu.SMEM)],
        out_specs=(vmem,) * 7,
        scratch_shapes=[
            pltpu.VMEM((points, scens), F32),
            ints, ints, ints,
            pltpu.VMEM((months, 8, scens), F32),
            pltpu.VMEM((8, 16), F32),
            pltpu.VMEM(base_table.shape, F32),
            pltpu.VMEM(shocks.shape, F32),
            pltpu.VMEM((1, scens), F32),
            pltpu.SMEM(fee_table.shape, F32),
            pltpu.SMEM(rollup_table.shape, F32),
            pltpu.SMEM((8,), F32),
            pltpu.VMEM((points, KDIM), BF16),
            pltpu.VMEM((KDIM, (months + 1) * scens), BF16),
            *[pltpu.VMEM((points, 2 * scens), BF16)] * 2,
            pltpu.VMEM((2, PLANE * (SHARE + BLOCK), points), BF16),
            pltpu.VMEM((2, PLANE, 8, 128), F32),
            pltpu.VMEM((2, PLANE - 1, 8, 128), F32),
            pltpu.VMEM((2, PLANE, ROWS, scens), F32),
            pltpu.VMEM((2, PLANE - 1, ROWS, scens), F32),
            pltpu.VMEM((PLANE * SHARE, 2 * scens), BF16),
            *[pltpu.VMEM((2, BLOCK * 8, PLANE * SHARE), BF16)] * 2,
            *[pltpu.VMEM((CHUNKS, PART, scens), F32)] * 3,
            pltpu.VMEM((16, 128), F32),
            pltpu.VMEM((RUN_Z - 1, 16, 128), F32),
            pltpu.VMEM((16, 128), F32),
            pltpu.VMEM((RING_Y - 1, 16, 128), F32),
            pltpu.VMEM((2 * RING_Y * 128, KDIM), BF16),
            pltpu.VMEM((BLOCK, scens), F32),
            dma((11,)),
            dma((blocks, 4)),
            *[dma((2, PLANE - 1))] * 4,
            *[dma((CHUNKS,))] * 2,
            *[dma((RUN_Z - 1,))] * 2,
            *[dma((RING_Y - 1,))] * 2,
            *[dma((CHUNKS, 2 * PLANE - 1))] * 2,
        ],
        compiler_params=pltpu.CompilerParams(
            collective_id=0, has_side_effects=True, vmem_limit_bytes=28 << 20
        ),
    )(*args, year_index)
    return pl.pallas_call(
        last_kernel,
        out_shape=(full, full, full, full, own),
        in_specs=[vmem] * 7,
        out_specs=(hbm,) * 5,
        scratch_shapes=[pltpu.VMEM((points, scens), F32), dma((4,)), dma((4,))],
        compiler_params=pltpu.CompilerParams(vmem_limit_bytes=28 << 20),
    )(*middle)


def solution(mesh):
    wide, row, last = P("proj", "scen"), P("proj"), P(None, None, "scen")
    placed = (
        wide, wide, wide, wide, row, row, row, last,
        P(), P(), P(), P(), P("scen"), last, P(), P(),
    )
    return jax.shard_map(
        body, mesh=mesh, in_specs=placed, out_specs=(wide,) * 5, check_vma=False
    )
```

time: 54.7 us -> 46.8 us (0.86)
  Pallas kernels: 50.5 us -> 44.8 us
  local copies, waits for them, and re-layouts: 2.48 us -> 0 us
    pallas_call x2, Pallas kernels: 50.5 us -> 44.8 us  [the longest x1 43.4 us: body(): pl.pallas_call(functools.partial(main_kernel, blocks), out_shape=(full, f...]
    unnamed x4 -> x0, local copies, waits for them, and re-layouts: 2.48 us -> none
where the time goes in v2:
time: 46.8 us; the launch traced here: 46.1 us
  Pallas kernels  44.8 us (96%)
  between operations  1.29 us (3%)
    pallas_call x1, Pallas kernels, body(): pl.pallas_call(functools.partial(main_kernel, blocks), out_shape=(full, f...  43.4 us
    pallas_call x1, Pallas kernels, body(): pl.pallas_call(last_kernel, out_shape=(full, full, full, full, own), in_s...  1.38 us

profile of v2, /device:TPU:1, one launch (start us, length us, event | category | flops | bytes accessed | tf_op | source)
XLA Modules:
  0.0 46.1 jit_solution(16704920460916789132)
XLA Ops:
  1.3 43.4 %shard_map.191 = (f32[1024,128]{1,0:T(8,128)S(1)}, f32[1024,128]{1,0:T(8,128)S(1)}, f32[1024,128]{1,0:T(8,128)S(1)}, bf16[1024,512]{1,0:T(8,128)(2,1)S(1)}, f32[...) custom-call(f32[1024,128]{1,0:T(8,128)} %fund.1, f32[1024,128]{1,0:T(8,128)} %force.1, ...), custom_call_target="tpu_custom_call" | custom-call | tf_op jit(solution)/shard_map/pallas_call | solution.py:469
  44.7 1.4 %shard_map.192 = (f32[1024,128]{1,0:T(8,128)}, f32[1024,128]{1,0:T(8,128)}, f32[1024,128]{1,0:T(8,128)}, f32[1024,128]{1,0:T(8,128)}, f32[32,128]{1,0:T(8,128)}) custom-call(f32[1024,128]{1,0:T(8,128)S(1)} %get-tuple-element.12.fund, f32[1024,128]{1,0:T(8,128)S(1)} %get-tuple-element.13.force, f32[1024,128]{1,0:T(8,128)S(1)} %get-tuple-element.14.base, ...), custom_call_target="tpu_custom_call" | custom-call | tf_op jit(solution)/shard_map/pallas_call | solution.py:520

commit v3 on v2

--- a/solution.py
+++ b/solution.py
@@ -66,12 +66,6 @@
     z_peers = [y * RUN_Z + lax.rem(zl + r, RUN_Z) for r in range(1, RUN_Z)]
     y_peers = [lax.rem(y + r, RING_Y) * RUN_Z + zl for r in range(1, RING_Y)]
 
-    barrier = pltpu.get_barrier_semaphore()
-    for p in [*far, across, *peers]:
-        pl.semaphore_signal(barrier, inc=1, device_id={"proj": p}, device_id_type=MESH)
-    for p in [*z_peers, *y_peers]:
-        pl.semaphore_signal(barrier, inc=1, device_id={"scen": p}, device_id_type=MESH)
-
     smalls = [
         pltpu.make_async_copy(src, dst, sem_small.at[n])
         for n, (src, dst) in enumerate((
@@ -95,12 +89,17 @@
     for i in range(blocks):
         for c in copies_in(i):
             c.start()
+
+    barrier = pltpu.get_barrier_semaphore()
+    for p in [*far, across, *peers]:
+        pl.semaphore_signal(barrier, inc=1, device_id={"proj": p}, device_id_type=MESH)
+    for p in [*z_peers, *y_peers]:
+        pl.semaphore_signal(barrier, inc=1, device_id={"scen": p}, device_id_type=MESH)
     for c in smalls:
         c.wait()
 
     lane = lax.broadcasted_iota(jnp.int32, (8, 128), 1)
     row8 = lax.broadcasted_iota(jnp.int32, (8, 128), 0)
-    row16 = lax.broadcasted_iota(jnp.int32, (16, points), 0)
 
     owners = points // SHARE
     coh_row = coh[...]
@@ -126,25 +125,36 @@
         [(coh_row - owner_row * BLOCK).astype(F32), prod_row.astype(F32)], points
     ).astype(BF16)
 
-    for k in range(2):
+    row16 = lax.broadcasted_iota(jnp.int32, (16, points), 0).astype(F32)
+    nil = jnp.zeros((16, points), BF16)
+
+    def tiled_hot(row):
+        tile = jnp.floor(row * 0.0625)
+        within = jnp.where(row16 == row - tile * 16.0, 1.0, 0.0).astype(BF16)
+        return jnp.broadcast_to(tile, (16, points)).astype(BF16), within
+
+    place_tile, place_hot = tiled_hot(place)
+    coh_tile, coh_hot = tiled_hot(coh_f)
+
+    def one_hots(k):
         plane = 1 - h if k == 0 else h
 
         def values(i, _):
-            want = (row16 + (plane * (PLANE * SHARE) + i * 16)).astype(F32)
+            tile = (plane * (PLANE * SHARE // 16) + i).astype(F32).astype(BF16)
             hot[k, pl.ds(pl.multiple_of(i * 16, 16), 16), :] = jnp.where(
-                place == want, 1.0, 0.0
-            ).astype(BF16)
+                place_tile == tile, place_hot, nil
+            )
             return 0
 
         def sums(i, _):
-            want = (row16 + (plane * (PLANE * BLOCK) + i * 16)).astype(F32)
+            tile = (plane * (PLANE * BLOCK // 16) + i).astype(F32).astype(BF16)
             hot[k, pl.ds(pl.multiple_of(PLANE * SHARE + i * 16, 16), 16), :] = jnp.where(
-                coh_f == want, 1.0, 0.0
-            ).astype(BF16)
+                coh_tile == tile, coh_hot, nil
+            )
             return 0
 
-        lax.fori_loop(0, PLANE * SHARE // 16, values, 0)
-        lax.fori_loop(0, PLANE * BLOCK // 16, sums, 0)
+        lax.fori_loop(0, PLANE * SHARE // 16, values, 0, unroll=4)
+        lax.fori_loop(0, PLANE * BLOCK // 16, sums, 0, unroll=4)
         lab = lax.dot_general(
             labels, hot[k, 0 : PLANE * SHARE, :], (((1,), (1,)), ((), ())),
             preferred_element_type=F32,
@@ -152,8 +162,10 @@
         for i in range(PLANE // 2):
             x = lab[:, i * 128 : (i + 1) * 128]
             back = pltpu.roll(x, 64, 1)
-            sl[k, 2 * i] = jnp.where(lane < 64, x, back)
-            sl[k, 2 * i + 1] = jnp.where(lane < 64, back, x)
+            sl[k, 2 * i] = jnp.where(lane < 64, x, back)[0:2]
+            sl[k, 2 * i + 1] = jnp.where(lane < 64, back, x)[0:2]
+
+    one_hots(0)
 
     products = mix.shape[1]
     m = mix[...]
@@ -207,23 +219,6 @@
             device_id={"scen": p}, device_id_type=MESH,
         )
 
-    pl.semaphore_wait(barrier, 2 * PLANE - 1 + len(z_peers) + len(y_peers))
-    l_sent = [[], []]
-    for k in range(2):
-        for r in range(1, PLANE):
-            l_sent[k].append(
-                to_proj(
-                    sl.at[k, lax.rem(u + r, PLANE)], rl.at[k, r - 1],
-                    l_s.at[k, r - 1], l_r.at[k, r - 1], peers[r - 1],
-                )
-            )
-            l_sent[k][-1].start()
-    a_sent = [
-        to_scen(p1s, p1r.at[r], a_s.at[r], a_r.at[r], z_peers[r]) for r in range(RUN_Z - 1)
-    ]
-    for c in a_sent:
-        c.start()
-
     step = 128
     for i in range(blocks):
         for c in copies_in(i):
@@ -250,8 +245,10 @@
             s_hi, s_lo = split2(n * b)
             ssv[at, 0:128], ssv[at, 128:256] = s_hi.astype(BF16), s_lo.astype(BF16)
 
-    x_sent = [[], []]
+    l_sent, x_sent, a_sent = [[], []], [[], []], []
     for k in range(2):
+        if k == 1:
+            one_hots(1)
         got = matmul(hot[k, 0 : PLANE * SHARE, :], wsv[...])
         for b in range(PLANE):
             part = got[b * SHARE : (b + 1) * SHARE]
@@ -260,14 +257,23 @@
         for b in range(PLANE):
             part = got[b * BLOCK : (b + 1) * BLOCK]
             sb[k, b, SHARE:, :] = part[:, :128] + part[:, 128:]
-        for r in range(1, PLANE):
-            x_sent[k].append(
-                to_proj(
-                    sb.at[k, lax.rem(u + r, PLANE)], rb.at[k, r - 1],
-                    x_s.at[k, r - 1], x_r.at[k, r - 1], peers[r - 1],
+        if k == 0:
+            pl.semaphore_wait(barrier, 2 * PLANE - 1 + len(z_peers) + len(y_peers))
+            a_sent = [
+                to_scen(p1s, p1r.at[r], a_s.at[r], a_r.at[r], z_peers[r])
+                for r in range(RUN_Z - 1)
+            ]
+            for c in a_sent:
+                c.start()
+        for src, dst, s, r, sent in ((sl, rl, l_s, l_r, l_sent), (sb, rb, x_s, x_r, x_sent)):
+            for n in range(PLANE - 1):
+                sent[k].append(
+                    to_proj(
+                        src.at[k, lax.rem(u + n + 1, PLANE)], dst.at[k, n],
+                        s.at[k, n], r.at[k, n], peers[n],
+                    )
                 )
-            )
-            x_sent[k][-1].start()
+                sent[k][-1].start()
 
     for c in a_sent:
         c.wait_recv()
@@ -284,7 +290,7 @@
             c.wait_recv()
         labs = [rl[k, n] for n in range(PLANE - 1)] + [sl[k, u]]
         lab = jnp.concatenate(
-            [jnp.where(lane < 64, labs[2 * i], labs[2 * i + 1]) for i in range(PLANE // 2)], axis=1
+            [jnp.where(lane[0:2] < 64, labs[2 * i], labs[2 * i + 1]) for i in range(PLANE // 2)], axis=1
         )
         here, which = lab[0:1, :], lab[1:2, :]
         arrived_hot = jnp.where(
@@ -304,7 +310,7 @@
                 ).astype(BF16)
             return 0
 
-        lax.fori_loop(0, BLOCK // 2, members, 0)
+        lax.fori_loop(0, BLOCK // 2, members, 0, unroll=4)
 
     def partial(k, dst):
         for c in x_sent[k]:
@@ -397,7 +403,7 @@
                 lfv[at, :] = factor[:, e * 128 : (e + 1) * 128]
             return 0
 
-        lax.fori_loop(0, CHUNK // 2, price, 0)
+        lax.fori_loop(0, CHUNK // 2, price, 0, unroll=2)
         for n, p in enumerate([*far, across, *peers]):
             c_sent.append(
                 to_proj(
@@ -492,8 +498,8 @@
             pltpu.VMEM((KDIM, (months + 1) * scens), BF16),
             *[pltpu.VMEM((points, 2 * scens), BF16)] * 2,
             pltpu.VMEM((2, PLANE * (SHARE + BLOCK), points), BF16),
-            pltpu.VMEM((2, PLANE, 8, 128), F32),
-            pltpu.VMEM((2, PLANE - 1, 8, 128), F32),
+            pltpu.VMEM((2, PLANE, 2, 128), F32),
+            pltpu.VMEM((2, PLANE - 1, 2, 128), F32),
             pltpu.VMEM((2, PLANE, ROWS, scens), F32),
             pltpu.VMEM((2, PLANE - 1, ROWS, scens), F32),
             pltpu.VMEM((PLANE * SHARE, 2 * scens), BF16),

time: 46.8 us -> 45.2 us (0.966); the launches traced: 46.1 us -> 45 us
  Pallas kernels: 44.8 us -> 43.7 us
    pallas_call x1, Pallas kernels: 43.4 us -> 42.4 us  [body(): pl.pallas_call(functools.partial(main_kernel, blocks), out_shape=(full, f...]
where the time goes in v3:
time: 45.2 us; the launch traced here: 45 us
  Pallas kernels  43.7 us (97%)
  between operations  1.29 us (3%)
    pallas_call x1, Pallas kernels, body(): pl.pallas_call(functools.partial(main_kernel, blocks), out_shape=(full, f...  42.4 us
    pallas_call x1, Pallas kernels, body(): pl.pallas_call(last_kernel, out_shape=(full, full, full, full, own), in_s...  1.38 us

profile of v3, /device:TPU:1, one launch (start us, length us, event | category | flops | bytes accessed | tf_op | source)
XLA Modules:
  0.0 45.0 jit_solution(4771466514659722366)
XLA Ops:
  1.3 42.4 %shard_map.191 = (f32[1024,128]{1,0:T(8,128)S(1)}, f32[1024,128]{1,0:T(8,128)S(1)}, f32[1024,128]{1,0:T(8,128)S(1)}, bf16[1024,512]{1,0:T(8,128)(2,1)S(1)}, f32[...) custom-call(f32[1024,128]{1,0:T(8,128)} %fund.1, f32[1024,128]{1,0:T(8,128)} %force.1, ...), custom_call_target="tpu_custom_call" | custom-call | tf_op jit(solution)/shard_map/pallas_call | solution.py:475
  43.6 1.4 %shard_map.192 = (f32[1024,128]{1,0:T(8,128)}, f32[1024,128]{1,0:T(8,128)}, f32[1024,128]{1,0:T(8,128)}, f32[1024,128]{1,0:T(8,128)}, f32[32,128]{1,0:T(8,128)}) custom-call(f32[1024,128]{1,0:T(8,128)S(1)} %get-tuple-element.12.fund, f32[1024,128]{1,0:T(8,128)S(1)} %get-tuple-element.13.force, f32[1024,128]{1,0:T(8,128)S(1)} %get-tuple-element.14.base, ...), custom_call_target="tpu_custom_call" | custom-call | tf_op jit(solution)/shard_map/pallas_call | solution.py:526

commit v4 on v3

--- a/solution.py
+++ b/solution.py
@@ -61,8 +61,13 @@
     h, u = lax.div(me, PLANE), lax.rem(me, PLANE)
     y, zl = lax.div(col, RUN_Z), lax.rem(col, RUN_Z)
     across = (1 - h) * PLANE + u
-    peers = [h * PLANE + lax.rem(u + r, PLANE) for r in range(1, PLANE)]
-    far = [(1 - h) * PLANE + lax.rem(u + r, PLANE) for r in range(1, PLANE)]
+    x, core = lax.div(u, 2), lax.rem(u, 2)
+    mates = [
+        lax.rem(x + dx, PLANE // 2) * 2 + (1 - core if dc else core)
+        for dx, dc in ((2, 0), (2, 1), (1, 0), (3, 0), (1, 1), (3, 1), (0, 1))
+    ]
+    peers = [h * PLANE + v for v in mates]
+    far = [(1 - h) * PLANE + v for v in mates]
     z_peers = [y * RUN_Z + lax.rem(zl + r, RUN_Z) for r in range(1, RUN_Z)]
     y_peers = [lax.rem(y + r, RING_Y) * RUN_Z + zl for r in range(1, RING_Y)]
 
@@ -91,7 +96,7 @@
             c.start()
 
     barrier = pltpu.get_barrier_semaphore()
-    for p in [*far, across, *peers]:
+    for p in [across, *peers]:
         pl.semaphore_signal(barrier, inc=1, device_id={"proj": p}, device_id_type=MESH)
     for p in [*z_peers, *y_peers]:
         pl.semaphore_signal(barrier, inc=1, device_id={"scen": p}, device_id_type=MESH)
@@ -258,7 +263,7 @@
             part = got[b * BLOCK : (b + 1) * BLOCK]
             sb[k, b, SHARE:, :] = part[:, :128] + part[:, 128:]
         if k == 0:
-            pl.semaphore_wait(barrier, 2 * PLANE - 1 + len(z_peers) + len(y_peers))
+            pl.semaphore_wait(barrier, PLANE + len(z_peers) + len(y_peers))
             a_sent = [
                 to_scen(p1s, p1r.at[r], a_s.at[r], a_r.at[r], z_peers[r])
                 for r in range(RUN_Z - 1)
@@ -269,7 +274,7 @@
             for n in range(PLANE - 1):
                 sent[k].append(
                     to_proj(
-                        src.at[k, lax.rem(u + n + 1, PLANE)], dst.at[k, n],
+                        src.at[k, mates[n]], dst.at[k, n],
                         s.at[k, n], r.at[k, n], peers[n],
                     )
                 )
@@ -285,7 +290,7 @@
         c.start()
 
     mix_pair = jnp.concatenate(split2(mix_norm), axis=0).astype(BF16)
-    for k in range(2):
+    def select_rows(k):
         for c in l_sent[k]:
             c.wait_recv()
         labs = [rl[k, n] for n in range(PLANE - 1)] + [sl[k, u]]
@@ -329,12 +334,15 @@
             dst[j, 0 : CHUNK * 8, :] = sums[j * CHUNK * 8 : (j + 1) * CHUNK * 8]
             dst[j, CHUNK * 8 :, :] = total[j * CHUNK : (j + 1) * CHUNK]
 
+    select_rows(0)
     partial(0, zs)
     z_sent = [
         to_proj(zs.at[j], zr.at[j], z_s.at[j], z_r.at[j], across) for j in range(CHUNKS)
     ]
     for c in z_sent:
         c.start()
+
+    select_rows(1)
 
     lapses = jnp.dot(
         table[...], prod_hot, precision=lax.Precision.HIGHEST, preferred_element_type=F32

time: 45.2 us -> 44.4 us (0.982)
  Pallas kernels: 43.7 us -> 43 us
    pallas_call x1, Pallas kernels: 42.4 us -> 41.6 us  [body(): pl.pallas_call(functools.partial(main_kernel, blocks), out_shape=(full, f...]
where the time goes in v4:
time: 44.4 us; the launch traced here: 44.3 us
  Pallas kernels  43 us (97%)
  between operations  1.29 us (3%)
    pallas_call x1, Pallas kernels, body(): pl.pallas_call(functools.partial(main_kernel, blocks), out_shape=(full, f...  41.6 us
    pallas_call x1, Pallas kernels, body(): pl.pallas_call(last_kernel, out_shape=(full, full, full, full, own), in_s...  1.38 us

profile of v4, /device:TPU:1, one launch (start us, length us, event | category | flops | bytes accessed | tf_op | source)
XLA Modules:
  0.0 44.3 jit_solution(7404632091148570698)
XLA Ops:
  1.3 41.6 %shard_map.191 = (f32[1024,128]{1,0:T(8,128)S(1)}, f32[1024,128]{1,0:T(8,128)S(1)}, f32[1024,128]{1,0:T(8,128)S(1)}, bf16[1024,512]{1,0:T(8,128)(2,1)S(1)}, f32[...) custom-call(f32[1024,128]{1,0:T(8,128)} %fund.1, f32[1024,128]{1,0:T(8,128)} %force.1, ...), custom_call_target="tpu_custom_call" | custom-call | tf_op jit(solution)/shard_map/pallas_call | solution.py:483
  42.9 1.4 %shard_map.192 = (f32[1024,128]{1,0:T(8,128)}, f32[1024,128]{1,0:T(8,128)}, f32[1024,128]{1,0:T(8,128)}, f32[1024,128]{1,0:T(8,128)}, f32[32,128]{1,0:T(8,128)}) custom-call(f32[1024,128]{1,0:T(8,128)S(1)} %get-tuple-element.12.fund, f32[1024,128]{1,0:T(8,128)S(1)} %get-tuple-element.13.force, f32[1024,128]{1,0:T(8,128)S(1)} %get-tuple-element.14.base, ...), custom_call_target="tpu_custom_call" | custom-call | tf_op jit(solution)/shard_map/pallas_call | solution.py:534

commit v5 on v4

--- a/solution.py
+++ b/solution.py
@@ -49,10 +49,10 @@
     fee_h, roll_h, vol_h, year,
     fund_o, force_o, base_o, pick, brow, cb, cost_o,
     lb, coh, prod, gtype, ret, mix, table, sh, sigma, fee, roll, vol,
-    lm, rm, wsv, ssv, hot, sl, rl, sb, rb, wmat, mh, ml, zs, zr, own,
+    lm, rm, wsv, ssv, hot, sl, rl, sb, rb, wmat, mh, ml, zs, zr, own, zx,
     p1s, p1r, p2s, p2r, lhs, lfv,
     sem_small, sem_in,
-    l_s, l_r, x_s, x_r, z_s, z_r, a_s, a_r, y_s, y_r, c_s, c_r,
+    l_s, l_r, x_s, x_r, z_s, z_r, a_s, a_r, y_s, y_r, c_s, c_r, e_s, e_r,
 ):
     points = lb.shape[0]
     size = points // blocks
@@ -368,6 +368,8 @@
             lhs[at : at + 128, :] = full.T.astype(BF16)
 
     partial(1, own)
+    e_sent = to_proj(own.at[CHUNKS - 1], zx, e_s.at[0], e_r.at[0], across)
+    e_sent.start()
 
     trials = RING_Y * 128
     vols = rows_of([vol[f] for f in range(8)], 128)
@@ -375,16 +377,22 @@
     level = sig * LOG2E
     drift = sig * sig * (-0.5 * LOG2E)
     c_sent = []
-    for j in range(CHUNKS):
-        z_sent[j].wait_recv()
+    for j in range(CHUNKS + 1):
+        both = j == CHUNKS
+        if both:
+            e_sent.wait_recv()
+            mine, other = zs.at[CHUNKS - 1], zx
+        else:
+            z_sent[j].wait_recv()
+            mine, other = own.at[j], zr.at[j]
 
         def price(i, _):
             tiles, money = [], []
             for e in range(2):
                 c = i * 2 + e
                 at = pl.ds(pl.multiple_of(c * 8, 8), 8)
-                s = own[j, at, :] + zr[j, at, :]
-                g = own[j, pl.ds(CHUNK * 8 + c, 1), :] + zr[j, pl.ds(CHUNK * 8 + c, 1), :]
+                s = mine[at, :] + other[at, :]
+                g = mine[pl.ds(CHUNK * 8 + c, 1), :] + other[pl.ds(CHUNK * 8 + c, 1), :]
                 inv = 1.0 / jnp.sum(s, axis=0, keepdims=True)
                 loads = s * inv * vols
                 d = drift * jnp.sum(loads * loads, axis=0, keepdims=True)
@@ -407,22 +415,31 @@
             factor = 0.3 + 2.0 / (1.0 + jnp.exp(5.0 * cost - 2.0))
             for e in range(2):
                 at = pl.ds(j * CHUNK + i * 2 + e, 1)
-                cost_o[at, :] = cost[:, e * 128 : (e + 1) * 128]
                 lfv[at, :] = factor[:, e * 128 : (e + 1) * 128]
+                if not both:
+                    cost_o[at, :] = cost[:, e * 128 : (e + 1) * 128]
             return 0
 
         lax.fori_loop(0, CHUNK // 2, price, 0, unroll=2)
-        for n, p in enumerate([*far, across, *peers]):
+        targets = [*peers, *far, across] if j < CHUNKS - 1 else peers
+        row = across * BLOCK + (j - 1) * CHUNK if both else me * BLOCK + j * CHUNK
+        if j < CHUNKS - 1:
+            order = [*range(PLANE - 1, 2 * PLANE - 1), *range(PLANE - 1)]
+        else:
+            order = range(PLANE - 1)
+        for n in order:
             c_sent.append(
                 to_proj(
                     lfv.at[pl.ds(j * CHUNK, CHUNK)],
-                    cb.at[pl.ds(pl.multiple_of(me * BLOCK + j * CHUNK, 8), CHUNK)],
-                    c_s.at[j, n], c_r.at[j, n], p,
+                    cb.at[pl.ds(pl.multiple_of(row, 8), CHUNK)],
+                    c_s.at[j, n], c_r.at[j, n], targets[n],
                 )
             )
             c_sent[-1].start()
 
-    cb[pl.ds(pl.multiple_of(me * BLOCK, 8), BLOCK), :] = lfv[...]
+    cb[pl.ds(pl.multiple_of(me * BLOCK, 8), BLOCK), :] = lfv[0:BLOCK, :]
+    cb[pl.ds(pl.multiple_of(across * BLOCK + BLOCK - CHUNK, 8), CHUNK), :] = lfv[BLOCK:, :]
+    e_sent.wait_send()
     for c in [*l_sent[0], *l_sent[1], *x_sent[0], *x_sent[1], *a_sent, *y_sent, *z_sent]:
         c.wait_send()
     for c in c_sent:
@@ -513,19 +530,21 @@
             pltpu.VMEM((PLANE * SHARE, 2 * scens), BF16),
             *[pltpu.VMEM((2, BLOCK * 8, PLANE * SHARE), BF16)] * 2,
             *[pltpu.VMEM((CHUNKS, PART, scens), F32)] * 3,
+            pltpu.VMEM((PART, scens), F32),
             pltpu.VMEM((16, 128), F32),
             pltpu.VMEM((RUN_Z - 1, 16, 128), F32),
             pltpu.VMEM((16, 128), F32),
             pltpu.VMEM((RING_Y - 1, 16, 128), F32),
             pltpu.VMEM((2 * RING_Y * 128, KDIM), BF16),
-            pltpu.VMEM((BLOCK, scens), F32),
+            pltpu.VMEM((BLOCK + CHUNK, scens), F32),
             dma((11,)),
             dma((blocks, 4)),
             *[dma((2, PLANE - 1))] * 4,
             *[dma((CHUNKS,))] * 2,
             *[dma((RUN_Z - 1,))] * 2,
             *[dma((RING_Y - 1,))] * 2,
-            *[dma((CHUNKS, 2 * PLANE - 1))] * 2,
+            *[dma((CHUNKS + 1, 2 * PLANE - 1))] * 2,
+            *[dma((1,))] * 2,
         ],
         compiler_params=pltpu.CompilerParams(
             collective_id=0, has_side_effects=True, vmem_limit_bytes=28 << 20

time: 44.4 us -> 43.8 us (0.986)
  Pallas kernels: 43 us -> 42.4 us
    pallas_call x1, Pallas kernels: 41.6 us -> 41 us  [body(): pl.pallas_call(functools.partial(main_kernel, blocks), out_shape=(full, f...]
where the time goes in v5:
time: 43.8 us; the launch traced here: 43.7 us
  Pallas kernels  42.4 us (97%)
  between operations  1.29 us (3%)
    pallas_call x1, Pallas kernels, body(): pl.pallas_call(functools.partial(main_kernel, blocks), out_shape=(full, f...  41 us
    pallas_call x1, Pallas kernels, body(): pl.pallas_call(last_kernel, out_shape=(full, full, full, full, own), in_s...  1.38 us

profile of v5, /device:TPU:1, one launch (start us, length us, event | category | flops | bytes accessed | tf_op | source)
XLA Modules:
  0.0 43.7 jit_solution(13277345953762866839)
XLA Ops:
  1.3 41.0 %shard_map.191 = (f32[1024,128]{1,0:T(8,128)S(1)}, f32[1024,128]{1,0:T(8,128)S(1)}, f32[1024,128]{1,0:T(8,128)S(1)}, bf16[1024,512]{1,0:T(8,128)(2,1)S(1)}, f32[...) custom-call(f32[1024,128]{1,0:T(8,128)} %fund.1, f32[1024,128]{1,0:T(8,128)} %force.1, ...), custom_call_target="tpu_custom_call" | custom-call | tf_op jit(solution)/shard_map/pallas_call | solution.py:500
  42.3 1.4 %shard_map.192 = (f32[1024,128]{1,0:T(8,128)}, f32[1024,128]{1,0:T(8,128)}, f32[1024,128]{1,0:T(8,128)}, f32[1024,128]{1,0:T(8,128)}, f32[32,128]{1,0:T(8,128)}) custom-call(f32[1024,128]{1,0:T(8,128)S(1)} %get-tuple-element.12.fund, f32[1024,128]{1,0:T(8,128)S(1)} %get-tuple-element.13.force, f32[1024,128]{1,0:T(8,128)S(1)} %get-tuple-element.14.base, ...), custom_call_target="tpu_custom_call" | custom-call | tf_op jit(solution)/shard_map/pallas_call | solution.py:553
